TPU v7x, 256 devices: a whole 4x4x8 slice. The times are simulated.
256 devices in a mesh: grp: 4 (over y), col: 64 (over x, z, core).
Axes of the slice: x: 4, y: 4, z: 8, core: 2. Of those that a mesh axis runs over, the one named last changes fastest.
Arguments:
- panels: bfloat16 [256, 4, 512, 512], P('col', None, 'grp'), may hold values from -1.296875 to 1.296875
- parent: float32 [256, 512, 512], P('col', 'grp'), may hold values from -6 to 6
- src_block: int32 [64, 40], P('col'), may hold values from 0 to 39, each once within a row
- dest_owner: int32 [2560, 1], P('col'), may hold values from 0 to 63; in each aligned block of 40 rows (0 to 39, 40 to 79, ...) no two rows name the same one
- target: int32 [2560], P('col'), may hold values from 0 to 3
- counts: int32 [64], P('col'), may hold values from 20 to 40, as said below
Outputs:
- assembled: float32 [256, 512, 512], P('col', 'grp')
Inputs may be any that keep to these rules, and one draw needn't show every extreme that they name: `src_block`: each row of a column rank is a permutation of the 40 block pairs. `dest_owner`: among the 40 slots of one column rank at most 1 name the same owner. The live slots of a rank are its first counts[c]; some rank has all 40 live.
All inputs are finite; a program needn't handle non-finite values.
Results may differ from a plain program's by a relative error of at most 0.0026.
Values may be sent and summed in bfloat16 or wider, within the bound.
No kernel may reach another device: no remote copies, remote signals or barrier semaphores. Data moves between devices by JAX's collectives and lax.ppermute only.
A program may use at most 128 MiB of HBM per device.

v0:
```python
import functools

import jax
import jax.numpy as jnp
from jax import lax
from jax.experimental import pallas as pl
from jax.experimental.pallas import tpu as pltpu
from jax.sharding import Mesh, PartitionSpec as P


NX, NZ, NC, NY = 4, 8, 2, 4
FRONTS, BLOCKS, ROWS, WIDTH = 4, 4, 128, 512
PAIRS, SLOTS, TARGETS = 10, 40, 4
COLS = 128
SPOTS = NX * NC * NZ
LABEL_ROWS = 16
PER_X = NC * NZ
SENT_ROWS = PER_X * ROWS + LABEL_ROWS
VMEM = 12 * 1024 * 1024
SUM_ROWS = TARGETS * ROWS
HOPS = NZ // 2


def products_kernel(place, src, owner, target, count, left, *rest, parts):
    rights, outs, (made, pair_at, label_at) = rest[:parts], rest[parts:parts + NX], rest[-3:]
    x, z, core = place[0], place[1], place[2]
    live = count[0]

    def clear(i, carry):
        pair_at[i] = SLOTS
        label_at[i] = -1
        return carry

    lax.fori_loop(0, SPOTS + 1, clear, 0)

    def put(s, carry):
        o = owner[s]
        dx = (o // (NZ * NC) - x + NX) % NX
        dz = ((o // NC) % NZ - z + NZ) % NZ
        dc = (o % NC - core + NC) % NC
        spot = jnp.where(s < live, (dx * NC + dc) * NZ + dz, SPOTS)
        pair_at[spot] = src[s]
        label_at[spot] = target[s]
        return carry

    lax.fori_loop(0, SLOTS, put, 0)

    def piece(f, b):
        if parts == 0:
            return left[f, b]
        return jnp.concatenate([r[f, b] for r in rights], axis=0)

    def front(f, carry):
        for b in range(0, BLOCKS, 2):
            mine = left[f, b:].reshape((BLOCKS - b) * ROWS, WIDTH)
            right = jnp.concatenate([piece(f, b), piece(f, b + 1)], axis=0)
            product = lax.dot_general(
                mine, right, (((1,), (1,)), ((), ())), preferred_element_type=jnp.float32
            ).astype(jnp.bfloat16)
            for c in (b, b + 1):
                for a in range(c, BLOCKS):
                    at = pl.multiple_of((f * PAIRS + a * (a + 1) // 2 + c) * ROWS, ROWS)
                    made[pl.ds(at, ROWS), :] = product[(a - b) * ROWS:(a - b + 1) * ROWS, (c - b) * COLS:(c - b + 1) * COLS]
        return carry

    lax.fori_loop(0, FRONTS, front, 0)
    made[SLOTS * ROWS:, :] = jnp.zeros((ROWS, COLS), jnp.bfloat16)
    row = lax.broadcasted_iota(jnp.int32, (LABEL_ROWS, COLS), 0)
    for dx, out in enumerate(outs):
        tile = jnp.full((LABEL_ROWS, COLS), -1, jnp.int32)
        for i in range(PER_X):
            tile = jnp.where(row == i, label_at[dx * PER_X + i], tile)
        out[PER_X * ROWS:, :] = tile.astype(jnp.float32).astype(jnp.bfloat16)

        def place_block(i, carry, dx=dx, out=out):
            at = pl.multiple_of(pair_at[dx * PER_X + i] * ROWS, ROWS)
            out[pl.ds(pl.multiple_of(i * ROWS, ROWS), ROWS), :] = made[pl.ds(at, ROWS), :]
            return carry

        lax.fori_loop(0, PER_X, place_block, 0)


def products(place, src, owner, target, count, left, rights):
    smem = pl.BlockSpec(memory_space=pltpu.SMEM)
    whole = pl.BlockSpec(memory_space=pltpu.VMEM)
    parts = len(rights)
    return pl.pallas_call(
        functools.partial(products_kernel, parts=parts),
        in_specs=[smem] * 5 + [whole] * (1 + parts),
        out_specs=[whole] * NX,
        out_shape=[jax.ShapeDtypeStruct((SENT_ROWS, COLS), jnp.bfloat16)] * NX,
        scratch_shapes=[
            pltpu.VMEM(((SLOTS + 1) * ROWS, COLS), jnp.bfloat16),
            pltpu.SMEM((SPOTS + 1,), jnp.int32),
            pltpu.SMEM((SPOTS + 1,), jnp.int32),
        ],
        compiler_params=pltpu.CompilerParams(vmem_limit_bytes=VMEM),
        cost_estimate=pl.CostEstimate(
            flops=2 * SLOTS * ROWS * COLS * WIDTH, bytes_accessed=6 * 1024 * 1024, transcendentals=0),
        name="products",
    )(place, src, owner, target, count, left, *rights)


def first_move(dc, dz):
    if dz % 2 == 0:
        return 2 * dc, dz // 2
    return (1, dz // 2) if dc == 0 else (3, (dz + 1) // 2 % HOPS)


def combine_kernel(*refs):
    arrived, outs = refs[:NX], refs[NX:]
    step = 32
    tags = [a[PER_X * ROWS:SENT_ROWS, :].astype(jnp.float32) for a in arrived]
    for i in range(PER_X):
        tag = [jnp.broadcast_to(t[i:i + 1, :], (step, COLS)) for t in tags]
        way, left = first_move(i // NZ, i % NZ)

        def rows_of(r, carry, i=i, tag=tag, out=outs[way], start=left * SUM_ROWS):
            base = pl.multiple_of(r * step, step)
            sums = [jnp.zeros((step, COLS), jnp.float32) for _ in range(TARGETS)]
            for g in range(NX):
                v = arrived[g][pl.ds(i * ROWS + base, step), :].astype(jnp.float32)
                for t in range(TARGETS):
                    sums[t] = sums[t] + jnp.where(tag[g] == float(t), v, 0.0)
            for t in range(TARGETS):
                out[pl.ds(start + t * ROWS + base, step), :] = sums[t].astype(jnp.bfloat16)
            return carry

        lax.fori_loop(0, ROWS // step, rows_of, 0)


def combine(arrived):
    whole = pl.BlockSpec(memory_space=pltpu.VMEM)
    return pl.pallas_call(
        combine_kernel,
        in_specs=[whole] * NX,
        out_specs=[whole] * 4,
        out_shape=[jax.ShapeDtypeStruct((HOPS * SUM_ROWS, COLS), jnp.bfloat16)] * 4,
        compiler_params=pltpu.CompilerParams(vmem_limit_bytes=VMEM),
        cost_estimate=pl.CostEstimate(
            flops=8 * SPOTS * ROWS * COLS, bytes_accessed=4 * 1024 * 1024, transcendentals=0),
        name="combine",
    )(*arrived)


def merge_kernel(*refs):
    parts, outs = refs[:4], refs[4:]
    step = 64
    for h, out in enumerate(outs):

        def rows_of(r, carry, h=h, out=out):
            base = pl.multiple_of(r * step, step)
            total = [p[pl.ds(h * SUM_ROWS + base, step), :].astype(jnp.float32) for p in parts]
            out[pl.ds(base, step), :] = (total[0] + total[1] + (total[2] + total[3])).astype(jnp.bfloat16)
            return carry

        lax.fori_loop(0, SUM_ROWS // step, rows_of, 0)


def merge(parts):
    whole = pl.BlockSpec(memory_space=pltpu.VMEM)
    return pl.pallas_call(
        merge_kernel,
        in_specs=[whole] * 4,
        out_specs=[whole] * HOPS,
        out_shape=[jax.ShapeDtypeStruct((SUM_ROWS, COLS), jnp.bfloat16)] * HOPS,
        compiler_params=pltpu.CompilerParams(vmem_limit_bytes=VMEM),
        cost_estimate=pl.CostEstimate(
            flops=4 * HOPS * SUM_ROWS * COLS, bytes_accessed=2 * 1024 * 1024, transcendentals=0),
        name="merge",
    )(*parts)


def block_sum(parts):
    total = parts[0][...].astype(jnp.float32)
    for p in parts[1:]:
        total = total + p[...].astype(jnp.float32)
    return total


def finish_kernel(piece, parent, *refs, sizes):
    out = refs[-1]
    sums, at = [], 0
    for n in sizes:
        sums.append(block_sum(refs[at:at + n]))
        at += n
    own, low, high = sums
    me, half = piece[0], COLS // 2
    values = {
        0: own,
        1: jnp.concatenate([low[:, :half], high[:, :half]], axis=1),
        2: None,
        3: jnp.concatenate([low[:, half:], high[:, half:]], axis=1),
    }
    for d, value in values.items():
        cols = pl.ds(pl.multiple_of(((me + d) % NY) * COLS, COLS), COLS)
        out[0, :, cols] = parent[0, :, cols] if value is None else parent[0, :, cols] - value


def finish(piece, parent, chunks):
    wide = pl.BlockSpec((1, ROWS, NY * COLS), lambda t: (t, 0, 0))
    flat = [part for chunk in chunks for part in chunk]
    return pl.pallas_call(
        functools.partial(finish_kernel, sizes=tuple(len(chunk) for chunk in chunks)),
        grid=(TARGETS,),
        in_specs=[pl.BlockSpec(memory_space=pltpu.SMEM), wide]
        + [pl.BlockSpec((ROWS, COLS), lambda t: (t, 0))] * len(flat),
        out_specs=wide,
        out_shape=jax.ShapeDtypeStruct(parent.shape, parent.dtype),
        compiler_params=pltpu.CompilerParams(
            dimension_semantics=("arbitrary",), vmem_limit_bytes=VMEM),
        cost_estimate=pl.CostEstimate(
            flops=30 * TARGETS * ROWS * COLS, bytes_accessed=5 * 1024 * 1024, transcendentals=0),
        name="finish",
    )(piece, parent, *flat)


def finish_last_kernel(piece, sofar, *refs):
    parts, (out, held, sem) = refs[:HOPS], refs[HOPS:]
    cols = pl.ds(pl.multiple_of((piece[0] + 2) % NY * COLS, COLS), COLS)
    load = pltpu.make_async_copy(sofar.at[:, :, cols], held, sem.at[0])
    load.start()
    load.wait()
    stores = []
    for t in range(TARGETS):
        held[t] = held[t] - block_sum([p.at[pl.ds(t * ROWS, ROWS)] for p in parts])
        stores.append(pltpu.make_async_copy(held.at[t], out.at[t, :, cols], sem.at[1 + t]))
        stores[-1].start()
    for c in stores:
        c.wait()


def finish_last(piece, sofar, chunk):
    hbm = pl.BlockSpec(memory_space=pl.ANY)
    return pl.pallas_call(
        finish_last_kernel,
        in_specs=[pl.BlockSpec(memory_space=pltpu.SMEM), hbm] + [pl.BlockSpec(memory_space=pltpu.VMEM)] * HOPS,
        out_specs=hbm,
        out_shape=jax.ShapeDtypeStruct(sofar.shape, sofar.dtype),
        scratch_shapes=[
            pltpu.VMEM((TARGETS, ROWS, COLS), jnp.float32),
            pltpu.SemaphoreType.DMA((1 + TARGETS,)),
        ],
        input_output_aliases={1: 0},
        compiler_params=pltpu.CompilerParams(vmem_limit_bytes=VMEM),
        cost_estimate=pl.CostEstimate(
            flops=10 * TARGETS * ROWS * COLS, bytes_accessed=2 * 1024 * 1024, transcendentals=0),
        name="finish_last",
    )(piece, sofar, *chunk)


def over_y(v, d):
    return lax.ppermute(v, "grp", [(i, (i + d) % NY) for i in range(NY)])


def over_x(v, dx):
    return lax.ppermute(v, "x", [(i, (i + dx) % NX) for i in range(NX)])


def over_z(v, dz, dc):
    pairs = [(z * NC + c, (z + dz) % NZ * NC + (c + dc) % NC) for z in range(NZ) for c in range(NC)]
    return lax.ppermute(v, ("z", "core"), pairs)


def per_device(panels, parent, src_block, dest_owner, target, counts):
    place = jnp.stack([lax.axis_index("x"), lax.axis_index("z"), lax.axis_index("core")]).astype(jnp.int32)
    piece = lax.axis_index("grp").astype(jnp.int32).reshape(1)
    slots = (place, src_block[0], dest_owner[:, 0], target, counts)
    half = ROWS // 2
    lower = panels[:, :, :half]
    upper = lax.optimization_barrier(panels)[:, :, half:]
    low_next, low_prev = over_y(lower, -1), over_y(lower, 1)
    up_next, up_prev = over_y(upper, -1), over_y(upper, 1)
    low_far = over_y(low_next, -1)
    up_far = over_y(up_prev, 1)
    rights = [(), (low_next, low_prev), (up_next, up_prev), (low_far, up_far)]
    summed = []
    for right in rights:
        packed = products(*slots, panels, right)
        arrived = [packed[0]] + [over_x(packed[d], d) for d in range(1, NX)]
        keep, plus, swap, cross = combine(arrived)
        parts = [keep, over_z(plus, 1, 0), over_z(swap, 0, 1), over_z(cross, -1, 1)]
        merged = merge(parts)
        summed.append([merged[0]] + [over_z(merged[h], 2 * h, 0) for h in range(1, HOPS)])
    sofar = finish(piece, parent, summed[:3])
    return finish_last(piece, sofar, summed[3])


def solution(mesh):
    split = Mesh(mesh.devices.reshape(NY, NX, NZ, NC), ("grp", "x", "z", "core"))
    col = ("x", "z", "core")
    placed = (
        P(col, None, "grp", None),
        P(col, "grp", None),
        P(col, None),
        P(col, None),
        P(col),
        P(col),
    )
    return jax.shard_map(
        per_device, mesh=split, in_specs=placed, out_specs=P(col, "grp", None), check_vma=False
    )
```

profile of v0, /device:TPU:1, one launch (start us, length us, event | category | flops | bytes accessed | tf_op | source)
XLA Modules:
  0.0 217.6 jit_solution(17363202095036857767)
XLA Ops:
  0.7 1.6 copy-done
  4.3 4.4 %products.4 = (bf16[2064,128]{1,0:T(8,128)(2,1)S(1)}, bf16[2064,128]{1,0:T(8,128)(2,1)S(1)}, bf16[2064,128]{1,0:T(8,128)(2,1)S(1)}, bf16[2064,128]{1,0:T(8,128)(2,1)S(1)}) custom-call(s32[3]{0:T(128)S(1)} %pad_add_fusion.place, s32[40]{0:T(128)S(1)} %bitcast.6, s32[40]{0:T(128)S(1)} %bitcast.10, s32[40]{0:T(128)S(1)} %copy-done.7, s32[1]{0:T(128)S(6)} %copy.9.count, ...), custom_call_target="tpu_custom_call" | custom-call | flops 671088640 | bytes 6291456 | tf_op jit(solution)/shard_map/products/pallas_call | solution.py:87
  8.7 2.1 collective-permute-start
  10.9 2.8 %collective-permute-start.9 = (bf16[4,4,64,512]{3,2,1,0:T(8,128)(2,1)S(1)}, bf16[4,4,64,512]{3,2,1,0:T(8,128)(2,1)S(1)}, u32[]{:S(2)}, u32[]{:S(2)}) collective-permute-start(bf16[4,4,64,512]{3,2,1,0:T(8,128)(2,1)S(1)} %slice.6), channel_id=1, source_target_pairs={{0,192},{64,0},{128,64},{192,128},{1,193},{65,1},{129,65},{193,129... | collective-permute-start | bytes 3145736 | tf_op jit(solution)/shard_map/ppermute | solution.py:253
  13.7 2.4 %collective-permute-start.1 = (bf16[2064,128]{1,0:T(8,128)(2,1)S(1)}, bf16[2064,128]{1,0:T(8,128)(2,1)S(1)}, u32[]{:S(2)}, u32[]{:S(2)}) collective-permute-start(bf16[2064,128]{1,0:T(8,128)(2,1)S(1)} %get-tuple-element.55), channel_id=1, source_target_pairs={{0,32},{16,48},{32,0},{48,16},{1,33},{17,49},{33,1},{49,17},{2,34}... | collective-permute-start | bytes 1585160 | tf_op jit(solution)/shard_map/ppermute | solution.py:257
  17.4 4.2 %collective-permute-done.refs_1_ = bf16[2064,128]{1,0:T(8,128)(2,1)S(1)} collective-permute-done((bf16[2064,128]{1,0:T(8,128)(2,1)S(1)}, bf16[2064,128]{1,0:T(8,128)(2,1)S(1)}, u32[]{:S(2)}, u32[]{:S(2)}) %collective-permute-start) | collective-permute-done | bytes 528416 | tf_op jit(solution)/shard_map/ppermute | solution.py:257
  21.7 3.4 %collective-permute-start.21 = (bf16[4,4,64,512]{3,2,1,0:T(8,128)(2,1)S(1)}, bf16[4,4,64,512]{3,2,1,0:T(8,128)(2,1)S(1)}, u32[]{:S(2)}, u32[]{:S(2)}) collective-permute-start(bf16[4,4,64,512]{3,2,1,0:T(8,128)(2,1)S(1)} %slice.8), channel_id=1, source_target_pairs={{0,64},{64,128},{128,192},{192,0},{1,65},{65,129},{129,193},{193,1... | collective-permute-start | bytes 3145736 | tf_op jit(solution)/shard_map/ppermute | solution.py:253
  25.0 11.0 %collective-permute-done.1.refs_2_ = bf16[2064,128]{1,0:T(8,128)(2,1)S(1)} collective-permute-done((bf16[2064,128]{1,0:T(8,128)(2,1)S(1)}, bf16[2064,128]{1,0:T(8,128)(2,1)S(1)}, u32[]{:S(2)}, u32[]{:S(2)}) %collective-permute-start.1) | collective-permute-done | bytes 528416 | tf_op jit(solution)/shard_map/ppermute | solution.py:257
  36.1 2.7 %collective-permute-start.20 = (bf16[4,4,64,512]{3,2,1,0:T(8,128)(2,1)S(1)}, bf16[4,4,64,512]{3,2,1,0:T(8,128)(2,1)S(1)}, u32[]{:S(2)}, u32[]{:S(2)}) collective-permute-start(bf16[4,4,64,512]{3,2,1,0:T(8,128)(2,1)S(1)} %slice.8), channel_id=1, source_target_pairs={{0,192},{64,0},{128,64},{192,128},{1,193},{65,1},{129,65},{193,129... | collective-permute-start | bytes 3145736 | tf_op jit(solution)/shard_map/ppermute | solution.py:253
  38.8 1.6 combine.4
  40.4 1.7 collective-permute-start.3
  42.1 2.1 collective-permute-start.4
  44.2 3.7 %collective-permute-start.5 = (bf16[2048,128]{1,0:T(8,128)(2,1)S(1)}, bf16[2048,128]{1,0:T(8,128)(2,1)S(1)}, u32[]{:S(2)}, u32[]{:S(2)}) collective-permute-start(bf16[2048,128]{1,0:T(8,128)(2,1)S(1)} %get-tuple-element.60), channel_id=1, source_target_pairs={{0,15},{1,14},{2,1},{3,0},{4,3},{5,2},{6,5},{7,4},{8,7},{9,6},{10,... | collective-permute-start | bytes 1572872 | tf_op jit(solution)/shard_map/ppermute | solution.py:262
  47.9 13.0 %collective-permute-done.21.rest_1_ = bf16[4,4,64,512]{3,2,1,0:T(8,128)(2,1)S(1)} collective-permute-done((bf16[4,4,64,512]{3,2,1,0:T(8,128)(2,1)S(1)}, bf16[4,4,64,512]{3,2,1,0:T(8,128)(2,1)S(1)}, u32[]{:S(2)}, u32[]{:S(2)}) %collective-permute-start.21) | collective-permute-done | bytes 1048608 | tf_op jit(solution)/shard_map/ppermute | solution.py:253
  60.9 1.5 collective-permute-start.32
  62.4 4.4 %products.5 = (bf16[2064,128]{1,0:T(8,128)(2,1)S(1)}, bf16[2064,128]{1,0:T(8,128)(2,1)S(1)}, bf16[2064,128]{1,0:T(8,128)(2,1)S(1)}, bf16[2064,128]{1,0:T(8,128)(2,1)S(1)}) custom-call(s32[3]{0:T(128)S(1)} %pad_add_fusion.place, s32[40]{0:T(128)S(1)} %bitcast.7, s32[40]{0:T(128)S(1)} %bitcast.11, s32[40]{0:T(128)S(1)} %copy-done.8, s32[1]{0:T(128)S(6)} %copy.9.count, ...), custom_call_target="tpu_custom_call" | custom-call | flops 671088640 | bytes 6291456 | tf_op jit(solution)/shard_map/products/pallas_call | solution.py:87
  68.1 1.4 collective-permute-start.12
  70.0 3.2 %collective-permute-start.6 = (bf16[512,128]{1,0:T(8,128)(2,1)S(1)}, bf16[512,128]{1,0:T(8,128)(2,1)S(1)}, u32[]{:S(2)}, u32[]{:S(2)}) collective-permute-start(bf16[512,128]{1,0:T(8,128)(2,1)S(1)} %get-tuple-element.62), channel_id=1, source_target_pairs={{0,4},{1,5},{2,6},{3,7},{4,8},{5,9},{6,10},{7,11},{8,12},{9,13},{1... | collective-permute-start | bytes 393224 | tf_op jit(solution)/shard_map/ppermute | solution.py:262
  73.3 5.5 %collective-permute-done.6.refs_1_ = bf16[512,128]{1,0:T(8,128)(2,1)S(1)} collective-permute-done((bf16[512,128]{1,0:T(8,128)(2,1)S(1)}, bf16[512,128]{1,0:T(8,128)(2,1)S(1)}, u32[]{:S(2)}, u32[]{:S(2)}) %collective-permute-start.6) | collective-permute-done | bytes 131104 | tf_op jit(solution)/shard_map/ppermute | solution.py:262
  78.8 2.1 collective-permute-start.13
  80.9 4.4 %products.6 = (bf16[2064,128]{1,0:T(8,128)(2,1)S(1)}, bf16[2064,128]{1,0:T(8,128)(2,1)S(1)}, bf16[2064,128]{1,0:T(8,128)(2,1)S(1)}, bf16[2064,128]{1,0:T(8,128)(2,1)S(1)}) custom-call(s32[3]{0:T(128)S(1)} %pad_add_fusion.place, s32[40]{0:T(128)S(1)} %bitcast.8, s32[40]{0:T(128)S(1)} %bitcast.12, s32[40]{0:T(128)S(1)} %copy-done.8, s32[1]{0:T(128)S(6)} %copy.9.count, ...), custom_call_target="tpu_custom_call" | custom-call | flops 671088640 | bytes 6291456 | tf_op jit(solution)/shard_map/products/pallas_call | solution.py:87
  85.4 4.9 %collective-permute-done.12.refs_2_ = bf16[2064,128]{1,0:T(8,128)(2,1)S(1)} collective-permute-done((bf16[2064,128]{1,0:T(8,128)(2,1)S(1)}, bf16[2064,128]{1,0:T(8,128)(2,1)S(1)}, u32[]{:S(2)}, u32[]{:S(2)}) %collective-permute-start.12) | collective-permute-done | bytes 528416 | tf_op jit(solution)/shard_map/ppermute | solution.py:257
  90.3 1.6 collective-permute-start.23
  91.9 7.0 %collective-permute-start.7 = (bf16[512,128]{1,0:T(8,128)(2,1)S(1)}, bf16[512,128]{1,0:T(8,128)(2,1)S(1)}, u32[]{:S(2)}, u32[]{:S(2)}) collective-permute-start(bf16[512,128]{1,0:T(8,128)(2,1)S(1)} %get-tuple-element.63), channel_id=1, source_target_pairs={{0,8},{1,9},{2,10},{3,11},{4,12},{5,13},{6,14},{7,15},{8,0},{9,1},... | collective-permute-start | bytes 393224 | tf_op jit(solution)/shard_map/ppermute | solution.py:262
  98.9 4.4 %products.7 = (bf16[2064,128]{1,0:T(8,128)(2,1)S(1)}, bf16[2064,128]{1,0:T(8,128)(2,1)S(1)}, bf16[2064,128]{1,0:T(8,128)(2,1)S(1)}, bf16[2064,128]{1,0:T(8,128)(2,1)S(1)}) custom-call(s32[3]{0:T(128)S(1)} %pad_add_fusion.place, s32[40]{0:T(128)S(1)} %bitcast.9, s32[40]{0:T(128)S(1)} %bitcast.13, s32[40]{0:T(128)S(1)} %copy-done.8, s32[1]{0:T(128)S(6)} %copy.9.count, ...), custom_call_target="tpu_custom_call" | custom-call | flops 671088640 | bytes 6291456 | tf_op jit(solution)/shard_map/products/pallas_call | solution.py:87
  103.4 1.4 collective-permute-start.33
  104.8 1.6 combine.5
  108.6 4.4 %collective-permute-done.23.refs_2_ = bf16[2064,128]{1,0:T(8,128)(2,1)S(1)} collective-permute-done((bf16[2064,128]{1,0:T(8,128)(2,1)S(1)}, bf16[2064,128]{1,0:T(8,128)(2,1)S(1)}, u32[]{:S(2)}, u32[]{:S(2)}) %collective-permute-start.23) | collective-permute-done | bytes 528416 | tf_op jit(solution)/shard_map/ppermute | solution.py:257
  113.0 1.5 collective-permute-done.24.refs_3_
  114.5 14.8 %collective-permute-start.15 = (bf16[2048,128]{1,0:T(8,128)(2,1)S(1)}, bf16[2048,128]{1,0:T(8,128)(2,1)S(1)}, u32[]{:S(2)}, u32[]{:S(2)}) collective-permute-start(bf16[2048,128]{1,0:T(8,128)(2,1)S(1)} %get-tuple-element.71), channel_id=1, source_target_pairs={{0,1},{1,0},{2,3},{3,2},{4,5},{5,4},{6,7},{7,6},{8,9},{9,8},{10,11... | collective-permute-start | bytes 1572872 | tf_op jit(solution)/shard_map/ppermute | solution.py:262
  129.3 1.6 combine.6
  130.9 5.0 %collective-permute-start.16 = (bf16[2048,128]{1,0:T(8,128)(2,1)S(1)}, bf16[2048,128]{1,0:T(8,128)(2,1)S(1)}, u32[]{:S(2)}, u32[]{:S(2)}) collective-permute-start(bf16[2048,128]{1,0:T(8,128)(2,1)S(1)} %get-tuple-element.72), channel_id=1, source_target_pairs={{0,15},{1,14},{2,1},{3,0},{4,3},{5,2},{6,5},{7,4},{8,7},{9,6},{10,... | collective-permute-start | bytes 1572872 | tf_op jit(solution)/shard_map/ppermute | solution.py:262
  135.9 3.3 %collective-permute-start.26 = (bf16[2048,128]{1,0:T(8,128)(2,1)S(1)}, bf16[2048,128]{1,0:T(8,128)(2,1)S(1)}, u32[]{:S(2)}, u32[]{:S(2)}) collective-permute-start(bf16[2048,128]{1,0:T(8,128)(2,1)S(1)} %get-tuple-element.83), channel_id=1, source_target_pairs={{0,1},{1,0},{2,3},{3,2},{4,5},{5,4},{6,7},{7,6},{8,9},{9,8},{10,11... | collective-permute-start | bytes 1572872 | tf_op jit(solution)/shard_map/ppermute | solution.py:262
  139.2 6.1 %collective-permute-start.27 = (bf16[2048,128]{1,0:T(8,128)(2,1)S(1)}, bf16[2048,128]{1,0:T(8,128)(2,1)S(1)}, u32[]{:S(2)}, u32[]{:S(2)}) collective-permute-start(bf16[2048,128]{1,0:T(8,128)(2,1)S(1)} %get-tuple-element.84), channel_id=1, source_target_pairs={{0,15},{1,14},{2,1},{3,0},{4,3},{5,2},{6,5},{7,4},{8,7},{9,6},{10,... | collective-permute-start | bytes 1572872 | tf_op jit(solution)/shard_map/ppermute | solution.py:262
  145.3 1.6 combine.7
  147.2 1.5 collective-permute-start.37
  150.0 2.1 collective-permute-start.38
  153.1 5.0 %collective-permute-done.27.refs_3_ = bf16[2048,128]{1,0:T(8,128)(2,1)S(1)} collective-permute-done((bf16[2048,128]{1,0:T(8,128)(2,1)S(1)}, bf16[2048,128]{1,0:T(8,128)(2,1)S(1)}, u32[]{:S(2)}, u32[]{:S(2)}) %collective-permute-start.27) | collective-permute-done | bytes 524320 | tf_op jit(solution)/shard_map/ppermute | solution.py:262
  159.7 15.3 %collective-permute-done.8.refs_3_ = bf16[512,128]{1,0:T(8,128)(2,1)S(1)} collective-permute-done((bf16[512,128]{1,0:T(8,128)(2,1)S(1)}, bf16[512,128]{1,0:T(8,128)(2,1)S(1)}, u32[]{:S(2)}, u32[]{:S(2)}) %collective-permute-start.8) | collective-permute-done | bytes 131104 | tf_op jit(solution)/shard_map/ppermute | solution.py:262
  175.0 4.5 %collective-permute-start.18 = (bf16[512,128]{1,0:T(8,128)(2,1)S(1)}, bf16[512,128]{1,0:T(8,128)(2,1)S(1)}, u32[]{:S(2)}, u32[]{:S(2)}) collective-permute-start(bf16[512,128]{1,0:T(8,128)(2,1)S(1)} %get-tuple-element.75), channel_id=1, source_target_pairs={{0,8},{1,9},{2,10},{3,11},{4,12},{5,13},{6,14},{7,15},{8,0},{9,1},... | collective-permute-start | bytes 393224 | tf_op jit(solution)/shard_map/ppermute | solution.py:262
  179.5 2.0 collective-permute-start.19
  181.9 2.9 %collective-permute-start.29 = (bf16[512,128]{1,0:T(8,128)(2,1)S(1)}, bf16[512,128]{1,0:T(8,128)(2,1)S(1)}, u32[]{:S(2)}, u32[]{:S(2)}) collective-permute-start(bf16[512,128]{1,0:T(8,128)(2,1)S(1)} %get-tuple-element.87), channel_id=1, source_target_pairs={{0,8},{1,9},{2,10},{3,11},{4,12},{5,13},{6,14},{7,15},{8,0},{9,1},... | collective-permute-start | bytes 393224 | tf_op jit(solution)/shard_map/ppermute | solution.py:262
  184.8 3.5 %collective-permute-start.30 = (bf16[512,128]{1,0:T(8,128)(2,1)S(1)}, bf16[512,128]{1,0:T(8,128)(2,1)S(1)}, u32[]{:S(2)}, u32[]{:S(2)}) collective-permute-start(bf16[512,128]{1,0:T(8,128)(2,1)S(1)} %get-tuple-element.88), channel_id=1, source_target_pairs={{0,12},{1,13},{2,14},{3,15},{4,0},{5,1},{6,2},{7,3},{8,4},{9,5},{1... | collective-permute-start | bytes 393224 | tf_op jit(solution)/shard_map/ppermute | solution.py:262
  189.4 2.9 %collective-permute-start.39 = (bf16[512,128]{1,0:T(8,128)(2,1)}, bf16[512,128]{1,0:T(8,128)(2,1)S(1)}, u32[]{:S(2)}, u32[]{:S(2)}) collective-permute-start(bf16[512,128]{1,0:T(8,128)(2,1)} %get-tuple-element.98), channel_id=1, source_target_pairs={{0,4},{1,5},{2,6},{3,7},{4,8},{5,9},{6,10},{7,11},{8,12},{9,13},{1... | collective-permute-start | bytes 393224 | tf_op jit(solution)/shard_map/ppermute | solution.py:262
  192.3 13.8 %collective-permute-done.19.refs_7_ = bf16[512,128]{1,0:T(8,128)(2,1)S(1)} collective-permute-done((bf16[512,128]{1,0:T(8,128)(2,1)S(1)}, bf16[512,128]{1,0:T(8,128)(2,1)S(1)}, u32[]{:S(2)}, u32[]{:S(2)}) %collective-permute-start.19) | collective-permute-done | bytes 131104 | tf_op jit(solution)/shard_map/ppermute | solution.py:262
  206.1 4.6 %collective-permute-start.40 = (bf16[512,128]{1,0:T(8,128)(2,1)}, bf16[512,128]{1,0:T(8,128)(2,1)S(1)}, u32[]{:S(2)}, u32[]{:S(2)}) collective-permute-start(bf16[512,128]{1,0:T(8,128)(2,1)} %get-tuple-element.99), channel_id=1, source_target_pairs={{0,8},{1,9},{2,10},{3,11},{4,12},{5,13},{6,14},{7,15},{8,0},{9,1},... | collective-permute-start | bytes 393224 | tf_op jit(solution)/shard_map/ppermute | solution.py:262
  211.6 1.8 finish.1.sofar
  215.7 1.7 finish_last.1
  (71 shorter events, 16.5 us)
Async XLA Ops:
  0.7 1.6 copy-start
  4.3 6.6 %copy-start.1 = (bf16[4,4,128,512]{3,2,1,0:T(8,128)(2,1)S(1)}, bf16[4,4,128,512]{3,2,1,0:T(8,128)(2,1)}, u32[]{:S(2)}) copy-start(bf16[4,4,128,512]{3,2,1,0:T(8,128)(2,1)} %left.7) | copy-start | bytes 6291460
  8.7 12.9 %collective-permute-start = (bf16[2064,128]{1,0:T(8,128)(2,1)S(1)}, bf16[2064,128]{1,0:T(8,128)(2,1)S(1)}, u32[]{:S(2)}, u32[]{:S(2)}) collective-permute-start(bf16[2064,128]{1,0:T(8,128)(2,1)S(1)} %get-tuple-element.54), channel_id=1, source_target_pairs={{0,16},{16,32},{32,48},{48,0},{1,17},{17,33},{33,49},{49,1},{2,18}... | collective-permute-start | bytes 1585160 | tf_op jit(solution)/shard_map/ppermute | solution.py:257
  10.9 31.2 %collective-permute-start.9 = (bf16[4,4,64,512]{3,2,1,0:T(8,128)(2,1)S(1)}, bf16[4,4,64,512]{3,2,1,0:T(8,128)(2,1)S(1)}, u32[]{:S(2)}, u32[]{:S(2)}) collective-permute-start(bf16[4,4,64,512]{3,2,1,0:T(8,128)(2,1)S(1)} %slice.6), channel_id=1, source_target_pairs={{0,192},{64,0},{128,64},{192,128},{1,193},{65,1},{129,65},{193,129... | collective-permute-start | bytes 3145736 | tf_op jit(solution)/shard_map/ppermute | solution.py:253
  13.7 30.5 %collective-permute-start.10 = (bf16[4,4,64,512]{3,2,1,0:T(8,128)(2,1)S(1)}, bf16[4,4,64,512]{3,2,1,0:T(8,128)(2,1)S(1)}, u32[]{:S(2)}, u32[]{:S(2)}) collective-permute-start(bf16[4,4,64,512]{3,2,1,0:T(8,128)(2,1)S(1)} %slice.6), channel_id=1, source_target_pairs={{0,64},{64,128},{128,192},{192,0},{1,65},{65,129},{129,193},{193,1... | collective-permute-start | bytes 3145736 | tf_op jit(solution)/shard_map/ppermute | solution.py:253
  13.7 22.3 %collective-permute-start.1 = (bf16[2064,128]{1,0:T(8,128)(2,1)S(1)}, bf16[2064,128]{1,0:T(8,128)(2,1)S(1)}, u32[]{:S(2)}, u32[]{:S(2)}) collective-permute-start(bf16[2064,128]{1,0:T(8,128)(2,1)S(1)} %get-tuple-element.55), channel_id=1, source_target_pairs={{0,32},{16,48},{32,0},{48,16},{1,33},{17,49},{33,1},{49,17},{2,34}... | collective-permute-start | bytes 1585160 | tf_op jit(solution)/shard_map/ppermute | solution.py:257
  16.2 46.2 %copy-start.4 = (s32[1,40]{1,0:T(1,128)S(1)}, s32[1,40]{1,0:T(1,128)}, u32[]{:S(2)}) copy-start(s32[1,40]{1,0:T(1,128)} %param.8) | copy-start | bytes 484
  16.2 46.2 %copy-start.6 = (s32[40,1]{0,1:T(1,128)S(1)}, s32[40,1]{0,1:T(1,128)}, u32[]{:S(2)}) copy-start(s32[40,1]{0,1:T(1,128)} %param.9) | copy-start | bytes 484
  16.2 46.2 %copy-start.8 = (s32[40]{0:T(128)S(1)}, s32[40]{0:T(128)}, u32[]{:S(2)}) copy-start(s32[40]{0:T(128)} %target.7) | copy-start | bytes 484
  16.2 22.6 %collective-permute-start.2 = (bf16[2064,128]{1,0:T(8,128)(2,1)S(1)}, bf16[2064,128]{1,0:T(8,128)(2,1)S(1)}, u32[]{:S(2)}, u32[]{:S(2)}) collective-permute-start(bf16[2064,128]{1,0:T(8,128)(2,1)S(1)} %get-tuple-element.56), channel_id=1, source_target_pairs={{0,48},{16,0},{32,16},{48,32},{1,49},{17,1},{33,17},{49,33},{2,50}... | collective-permute-start | bytes 1585160 | tf_op jit(solution)/shard_map/ppermute | solution.py:257
  21.7 39.3 %collective-permute-start.21 = (bf16[4,4,64,512]{3,2,1,0:T(8,128)(2,1)S(1)}, bf16[4,4,64,512]{3,2,1,0:T(8,128)(2,1)S(1)}, u32[]{:S(2)}, u32[]{:S(2)}) collective-permute-start(bf16[4,4,64,512]{3,2,1,0:T(8,128)(2,1)S(1)} %slice.8), channel_id=1, source_target_pairs={{0,64},{64,128},{128,192},{192,0},{1,65},{65,129},{129,193},{193,1... | collective-permute-start | bytes 3145736 | tf_op jit(solution)/shard_map/ppermute | solution.py:253
  36.1 34.0 %collective-permute-start.20 = (bf16[4,4,64,512]{3,2,1,0:T(8,128)(2,1)S(1)}, bf16[4,4,64,512]{3,2,1,0:T(8,128)(2,1)S(1)}, u32[]{:S(2)}, u32[]{:S(2)}) collective-permute-start(bf16[4,4,64,512]{3,2,1,0:T(8,128)(2,1)S(1)} %slice.8), channel_id=1, source_target_pairs={{0,192},{64,0},{128,64},{192,128},{1,193},{65,1},{129,65},{193,129... | collective-permute-start | bytes 3145736 | tf_op jit(solution)/shard_map/ppermute | solution.py:253
  40.4 20.5 %collective-permute-start.3 = (bf16[2048,128]{1,0:T(8,128)(2,1)S(1)}, bf16[2048,128]{1,0:T(8,128)(2,1)S(1)}, u32[]{:S(2)}, u32[]{:S(2)}) collective-permute-start(bf16[2048,128]{1,0:T(8,128)(2,1)S(1)} %get-tuple-element.58), channel_id=1, source_target_pairs={{0,2},{1,3},{2,4},{3,5},{4,6},{5,7},{6,8},{7,9},{8,10},{9,11},{10,... | collective-permute-start | bytes 1572872 | tf_op jit(solution)/shard_map/ppermute | solution.py:262
  42.1 24.7 %collective-permute-start.4 = (bf16[2048,128]{1,0:T(8,128)(2,1)S(1)}, bf16[2048,128]{1,0:T(8,128)(2,1)S(1)}, u32[]{:S(2)}, u32[]{:S(2)}) collective-permute-start(bf16[2048,128]{1,0:T(8,128)(2,1)S(1)} %get-tuple-element.59), channel_id=1, source_target_pairs={{0,1},{1,0},{2,3},{3,2},{4,5},{5,4},{6,7},{7,6},{8,9},{9,8},{10,11... | collective-permute-start | bytes 1572872 | tf_op jit(solution)/shard_map/ppermute | solution.py:262
  44.2 23.9 %collective-permute-start.5 = (bf16[2048,128]{1,0:T(8,128)(2,1)S(1)}, bf16[2048,128]{1,0:T(8,128)(2,1)S(1)}, u32[]{:S(2)}, u32[]{:S(2)}) collective-permute-start(bf16[2048,128]{1,0:T(8,128)(2,1)S(1)} %get-tuple-element.60), channel_id=1, source_target_pairs={{0,15},{1,14},{2,1},{3,0},{4,3},{5,2},{6,5},{7,4},{8,7},{9,6},{10,... | collective-permute-start | bytes 1572872 | tf_op jit(solution)/shard_map/ppermute | solution.py:262
  60.9 31.0 %collective-permute-start.31 = (bf16[4,4,64,512]{3,2,1,0:T(8,128)(2,1)S(1)}, bf16[4,4,64,512]{3,2,1,0:T(8,128)(2,1)S(1)}, u32[]{:S(2)}, u32[]{:S(2)}) collective-permute-start(bf16[4,4,64,512]{3,2,1,0:T(8,128)(2,1)S(1)} %collective-permute-done.9.rest_0_), channel_id=1, source_target_pairs={{0,192},{64,0},{128,64},{192,128},{1,193},{65,1},{129,65},{193,129... | collective-permute-start | bytes 3145736 | tf_op jit(solution)/shard_map/ppermute | solution.py:253
  60.9 31.0 %collective-permute-start.32 = (bf16[4,4,64,512]{3,2,1,0:T(8,128)(2,1)S(1)}, bf16[4,4,64,512]{3,2,1,0:T(8,128)(2,1)S(1)}, u32[]{:S(2)}, u32[]{:S(2)}) collective-permute-start(bf16[4,4,64,512]{3,2,1,0:T(8,128)(2,1)S(1)} %collective-permute-done.21.rest_1_), channel_id=1, source_target_pairs={{0,64},{64,128},{128,192},{192,0},{1,65},{65,129},{129,193},{193,1... | collective-permute-start | bytes 3145736 | tf_op jit(solution)/shard_map/ppermute | solution.py:253
  66.8 18.5 %collective-permute-start.11 = (bf16[2064,128]{1,0:T(8,128)(2,1)S(1)}, bf16[2064,128]{1,0:T(8,128)(2,1)S(1)}, u32[]{:S(2)}, u32[]{:S(2)}) collective-permute-start(bf16[2064,128]{1,0:T(8,128)(2,1)S(1)} %get-tuple-element.66), channel_id=1, source_target_pairs={{0,16},{16,32},{32,48},{48,0},{1,17},{17,33},{33,49},{49,1},{2,18}... | collective-permute-start | bytes 1585160 | tf_op jit(solution)/shard_map/ppermute | solution.py:257
  68.1 22.2 %collective-permute-start.12 = (bf16[2064,128]{1,0:T(8,128)(2,1)S(1)}, bf16[2064,128]{1,0:T(8,128)(2,1)S(1)}, u32[]{:S(2)}, u32[]{:S(2)}) collective-permute-start(bf16[2064,128]{1,0:T(8,128)(2,1)S(1)} %get-tuple-element.67), channel_id=1, source_target_pairs={{0,32},{16,48},{32,0},{48,16},{1,33},{17,49},{33,1},{49,17},{2,34}... | collective-permute-start | bytes 1585160 | tf_op jit(solution)/shard_map/ppermute | solution.py:257
  70.0 8.8 %collective-permute-start.6 = (bf16[512,128]{1,0:T(8,128)(2,1)S(1)}, bf16[512,128]{1,0:T(8,128)(2,1)S(1)}, u32[]{:S(2)}, u32[]{:S(2)}) collective-permute-start(bf16[512,128]{1,0:T(8,128)(2,1)S(1)} %get-tuple-element.62), channel_id=1, source_target_pairs={{0,4},{1,5},{2,6},{3,7},{4,8},{5,9},{6,10},{7,11},{8,12},{9,13},{1... | collective-permute-start | bytes 393224 | tf_op jit(solution)/shard_map/ppermute | solution.py:262
  78.8 24.6 %collective-permute-start.13 = (bf16[2064,128]{1,0:T(8,128)(2,1)S(1)}, bf16[2064,128]{1,0:T(8,128)(2,1)S(1)}, u32[]{:S(2)}, u32[]{:S(2)}) collective-permute-start(bf16[2064,128]{1,0:T(8,128)(2,1)S(1)} %get-tuple-element.68), channel_id=1, source_target_pairs={{0,48},{16,0},{32,16},{48,32},{1,49},{17,1},{33,17},{49,33},{2,50}... | collective-permute-start | bytes 1585160 | tf_op jit(solution)/shard_map/ppermute | solution.py:257
  85.3 21.9 %collective-permute-start.22 = (bf16[2064,128]{1,0:T(8,128)(2,1)S(1)}, bf16[2064,128]{1,0:T(8,128)(2,1)S(1)}, u32[]{:S(2)}, u32[]{:S(2)}) collective-permute-start(bf16[2064,128]{1,0:T(8,128)(2,1)S(1)} %get-tuple-element.78), channel_id=1, source_target_pairs={{0,16},{16,32},{32,48},{48,0},{1,17},{17,33},{33,49},{49,1},{2,18}... | collective-permute-start | bytes 1585160 | tf_op jit(solution)/shard_map/ppermute | solution.py:257
  90.3 22.7 %collective-permute-start.23 = (bf16[2064,128]{1,0:T(8,128)(2,1)S(1)}, bf16[2064,128]{1,0:T(8,128)(2,1)S(1)}, u32[]{:S(2)}, u32[]{:S(2)}) collective-permute-start(bf16[2064,128]{1,0:T(8,128)(2,1)S(1)} %get-tuple-element.79), channel_id=1, source_target_pairs={{0,32},{16,48},{32,0},{48,16},{1,33},{17,49},{33,1},{49,17},{2,34}... | collective-permute-start | bytes 1585160 | tf_op jit(solution)/shard_map/ppermute | solution.py:257
  91.9 22.6 %collective-permute-start.24 = (bf16[2064,128]{1,0:T(8,128)(2,1)S(1)}, bf16[2064,128]{1,0:T(8,128)(2,1)S(1)}, u32[]{:S(2)}, u32[]{:S(2)}) collective-permute-start(bf16[2064,128]{1,0:T(8,128)(2,1)S(1)} %get-tuple-element.80), channel_id=1, source_target_pairs={{0,48},{16,0},{32,16},{48,32},{1,49},{17,1},{33,17},{49,33},{2,50}... | collective-permute-start | bytes 1585160 | tf_op jit(solution)/shard_map/ppermute | solution.py:257
  91.9 14.5 %collective-permute-start.7 = (bf16[512,128]{1,0:T(8,128)(2,1)S(1)}, bf16[512,128]{1,0:T(8,128)(2,1)S(1)}, u32[]{:S(2)}, u32[]{:S(2)}) collective-permute-start(bf16[512,128]{1,0:T(8,128)(2,1)S(1)} %get-tuple-element.63), channel_id=1, source_target_pairs={{0,8},{1,9},{2,10},{3,11},{4,12},{5,13},{6,14},{7,15},{8,0},{9,1},... | collective-permute-start | bytes 393224 | tf_op jit(solution)/shard_map/ppermute | solution.py:262
  103.4 32.5 %collective-permute-start.33 = (bf16[2064,128]{1,0:T(8,128)(2,1)S(1)}, bf16[2064,128]{1,0:T(8,128)(2,1)S(1)}, u32[]{:S(2)}, u32[]{:S(2)}) collective-permute-start(bf16[2064,128]{1,0:T(8,128)(2,1)S(1)} %get-tuple-element.90), channel_id=1, source_target_pairs={{0,16},{16,32},{32,48},{48,0},{1,17},{17,33},{33,49},{49,1},{2,18}... | collective-permute-start | bytes 1585160 | tf_op jit(solution)/shard_map/ppermute | solution.py:257
  106.4 24.5 %collective-permute-start.14 = (bf16[2048,128]{1,0:T(8,128)(2,1)S(1)}, bf16[2048,128]{1,0:T(8,128)(2,1)S(1)}, u32[]{:S(2)}, u32[]{:S(2)}) collective-permute-start(bf16[2048,128]{1,0:T(8,128)(2,1)S(1)} %get-tuple-element.70), channel_id=1, source_target_pairs={{0,2},{1,3},{2,4},{3,5},{4,6},{5,7},{6,8},{7,9},{8,10},{9,11},{10,... | collective-permute-start | bytes 1572872 | tf_op jit(solution)/shard_map/ppermute | solution.py:262
  107.2 28.6 %collective-permute-start.34 = (bf16[2064,128]{1,0:T(8,128)(2,1)S(1)}, bf16[2064,128]{1,0:T(8,128)(2,1)S(1)}, u32[]{:S(2)}, u32[]{:S(2)}) collective-permute-start(bf16[2064,128]{1,0:T(8,128)(2,1)S(1)} %get-tuple-element.91), channel_id=1, source_target_pairs={{0,32},{16,48},{32,0},{48,16},{1,33},{17,49},{33,1},{49,17},{2,34}... | collective-permute-start | bytes 1585160 | tf_op jit(solution)/shard_map/ppermute | solution.py:257
  113.0 26.2 %collective-permute-start.35 = (bf16[2064,128]{1,0:T(8,128)(2,1)S(1)}, bf16[2064,128]{1,0:T(8,128)(2,1)S(1)}, u32[]{:S(2)}, u32[]{:S(2)}) collective-permute-start(bf16[2064,128]{1,0:T(8,128)(2,1)S(1)} %get-tuple-element.92), channel_id=1, source_target_pairs={{0,48},{16,0},{32,16},{48,32},{1,49},{17,1},{33,17},{49,33},{2,50}... | collective-permute-start | bytes 1585160 | tf_op jit(solution)/shard_map/ppermute | solution.py:257
  114.5 32.4 %collective-permute-start.15 = (bf16[2048,128]{1,0:T(8,128)(2,1)S(1)}, bf16[2048,128]{1,0:T(8,128)(2,1)S(1)}, u32[]{:S(2)}, u32[]{:S(2)}) collective-permute-start(bf16[2048,128]{1,0:T(8,128)(2,1)S(1)} %get-tuple-element.71), channel_id=1, source_target_pairs={{0,1},{1,0},{2,3},{3,2},{4,5},{5,4},{6,7},{7,6},{8,9},{9,8},{10,11... | collective-permute-start | bytes 1572872 | tf_op jit(solution)/shard_map/ppermute | solution.py:262
  130.9 16.3 %collective-permute-start.16 = (bf16[2048,128]{1,0:T(8,128)(2,1)S(1)}, bf16[2048,128]{1,0:T(8,128)(2,1)S(1)}, u32[]{:S(2)}, u32[]{:S(2)}) collective-permute-start(bf16[2048,128]{1,0:T(8,128)(2,1)S(1)} %get-tuple-element.72), channel_id=1, source_target_pairs={{0,15},{1,14},{2,1},{3,0},{4,3},{5,2},{6,5},{7,4},{8,7},{9,6},{10,... | collective-permute-start | bytes 1572872 | tf_op jit(solution)/shard_map/ppermute | solution.py:262
  135.8 14.2 %collective-permute-start.25 = (bf16[2048,128]{1,0:T(8,128)(2,1)S(1)}, bf16[2048,128]{1,0:T(8,128)(2,1)S(1)}, u32[]{:S(2)}, u32[]{:S(2)}) collective-permute-start(bf16[2048,128]{1,0:T(8,128)(2,1)S(1)} %get-tuple-element.82), channel_id=1, source_target_pairs={{0,2},{1,3},{2,4},{3,5},{4,6},{5,7},{6,8},{7,9},{8,10},{9,11},{10,... | collective-permute-start | bytes 1572872 | tf_op jit(solution)/shard_map/ppermute | solution.py:262
  135.9 16.7 %collective-permute-start.26 = (bf16[2048,128]{1,0:T(8,128)(2,1)S(1)}, bf16[2048,128]{1,0:T(8,128)(2,1)S(1)}, u32[]{:S(2)}, u32[]{:S(2)}) collective-permute-start(bf16[2048,128]{1,0:T(8,128)(2,1)S(1)} %get-tuple-element.83), channel_id=1, source_target_pairs={{0,1},{1,0},{2,3},{3,2},{4,5},{5,4},{6,7},{7,6},{8,9},{9,8},{10,11... | collective-permute-start | bytes 1572872 | tf_op jit(solution)/shard_map/ppermute | solution.py:262
  139.2 19.0 %collective-permute-start.27 = (bf16[2048,128]{1,0:T(8,128)(2,1)S(1)}, bf16[2048,128]{1,0:T(8,128)(2,1)S(1)}, u32[]{:S(2)}, u32[]{:S(2)}) collective-permute-start(bf16[2048,128]{1,0:T(8,128)(2,1)S(1)} %get-tuple-element.84), channel_id=1, source_target_pairs={{0,15},{1,14},{2,1},{3,0},{4,3},{5,2},{6,5},{7,4},{8,7},{9,6},{10,... | collective-permute-start | bytes 1572872 | tf_op jit(solution)/shard_map/ppermute | solution.py:262
  146.9 34.6 %collective-permute-start.36 = (bf16[2048,128]{1,0:T(8,128)(2,1)S(1)}, bf16[2048,128]{1,0:T(8,128)(2,1)S(1)}, u32[]{:S(2)}, u32[]{:S(2)}) collective-permute-start(bf16[2048,128]{1,0:T(8,128)(2,1)S(1)} %get-tuple-element.94), channel_id=1, source_target_pairs={{0,2},{1,3},{2,4},{3,5},{4,6},{5,7},{6,8},{7,9},{8,10},{9,11},{10,... | collective-permute-start | bytes 1572872 | tf_op jit(solution)/shard_map/ppermute | solution.py:262
  147.2 34.7 %collective-permute-start.37 = (bf16[2048,128]{1,0:T(8,128)(2,1)S(1)}, bf16[2048,128]{1,0:T(8,128)(2,1)S(1)}, u32[]{:S(2)}, u32[]{:S(2)}) collective-permute-start(bf16[2048,128]{1,0:T(8,128)(2,1)S(1)} %get-tuple-element.95), channel_id=1, source_target_pairs={{0,1},{1,0},{2,3},{3,2},{4,5},{5,4},{6,7},{7,6},{8,9},{9,8},{10,11... | collective-permute-start | bytes 1572872 | tf_op jit(solution)/shard_map/ppermute | solution.py:262
  150.0 34.7 %collective-permute-start.38 = (bf16[2048,128]{1,0:T(8,128)(2,1)S(1)}, bf16[2048,128]{1,0:T(8,128)(2,1)S(1)}, u32[]{:S(2)}, u32[]{:S(2)}) collective-permute-start(bf16[2048,128]{1,0:T(8,128)(2,1)S(1)} %get-tuple-element.96), channel_id=1, source_target_pairs={{0,15},{1,14},{2,1},{3,0},{4,3},{5,2},{6,5},{7,4},{8,7},{9,6},{10,... | collective-permute-start | bytes 1572872 | tf_op jit(solution)/shard_map/ppermute | solution.py:262
  152.6 22.4 %collective-permute-start.8 = (bf16[512,128]{1,0:T(8,128)(2,1)S(1)}, bf16[512,128]{1,0:T(8,128)(2,1)S(1)}, u32[]{:S(2)}, u32[]{:S(2)}) collective-permute-start(bf16[512,128]{1,0:T(8,128)(2,1)S(1)} %get-tuple-element.64), channel_id=1, source_target_pairs={{0,12},{1,13},{2,14},{3,15},{4,0},{5,1},{6,2},{7,3},{8,4},{9,5},{1... | collective-permute-start | bytes 393224 | tf_op jit(solution)/shard_map/ppermute | solution.py:262
  158.1 21.4 %collective-permute-start.17 = (bf16[512,128]{1,0:T(8,128)(2,1)S(1)}, bf16[512,128]{1,0:T(8,128)(2,1)S(1)}, u32[]{:S(2)}, u32[]{:S(2)}) collective-permute-start(bf16[512,128]{1,0:T(8,128)(2,1)S(1)} %get-tuple-element.74), channel_id=1, source_target_pairs={{0,4},{1,5},{2,6},{3,7},{4,8},{5,9},{6,10},{7,11},{8,12},{9,13},{1... | collective-permute-start | bytes 393224 | tf_op jit(solution)/shard_map/ppermute | solution.py:262
  159.2 52.4 %copy-start.2 = (f32[4,128,512]{2,1,0:T(8,128)S(1)}, f32[4,128,512]{2,1,0:T(8,128)}, u32[]{:S(2)}) copy-start(f32[4,128,512]{2,1,0:T(8,128)} %parent.1) | copy-start | bytes 3145732
  175.0 14.5 %collective-permute-start.18 = (bf16[512,128]{1,0:T(8,128)(2,1)S(1)}, bf16[512,128]{1,0:T(8,128)(2,1)S(1)}, u32[]{:S(2)}, u32[]{:S(2)}) collective-permute-start(bf16[512,128]{1,0:T(8,128)(2,1)S(1)} %get-tuple-element.75), channel_id=1, source_target_pairs={{0,8},{1,9},{2,10},{3,11},{4,12},{5,13},{6,14},{7,15},{8,0},{9,1},... | collective-permute-start | bytes 393224 | tf_op jit(solution)/shard_map/ppermute | solution.py:262
  179.5 26.6 %collective-permute-start.19 = (bf16[512,128]{1,0:T(8,128)(2,1)S(1)}, bf16[512,128]{1,0:T(8,128)(2,1)S(1)}, u32[]{:S(2)}, u32[]{:S(2)}) collective-permute-start(bf16[512,128]{1,0:T(8,128)(2,1)S(1)} %get-tuple-element.76), channel_id=1, source_target_pairs={{0,12},{1,13},{2,14},{3,15},{4,0},{5,1},{6,2},{7,3},{8,4},{9,5},{1... | collective-permute-start | bytes 393224 | tf_op jit(solution)/shard_map/ppermute | solution.py:262
  181.5 29.2 %collective-permute-start.28 = (bf16[512,128]{1,0:T(8,128)(2,1)S(1)}, bf16[512,128]{1,0:T(8,128)(2,1)S(1)}, u32[]{:S(2)}, u32[]{:S(2)}) collective-permute-start(bf16[512,128]{1,0:T(8,128)(2,1)S(1)} %get-tuple-element.86), channel_id=1, source_target_pairs={{0,4},{1,5},{2,6},{3,7},{4,8},{5,9},{6,10},{7,11},{8,12},{9,13},{1... | collective-permute-start | bytes 393224 | tf_op jit(solution)/shard_map/ppermute | solution.py:262
  181.9 29.7 %collective-permute-start.29 = (bf16[512,128]{1,0:T(8,128)(2,1)S(1)}, bf16[512,128]{1,0:T(8,128)(2,1)S(1)}, u32[]{:S(2)}, u32[]{:S(2)}) collective-permute-start(bf16[512,128]{1,0:T(8,128)(2,1)S(1)} %get-tuple-element.87), channel_id=1, source_target_pairs={{0,8},{1,9},{2,10},{3,11},{4,12},{5,13},{6,14},{7,15},{8,0},{9,1},... | collective-permute-start | bytes 393224 | tf_op jit(solution)/shard_map/ppermute | solution.py:262
  184.8 26.8 %collective-permute-start.30 = (bf16[512,128]{1,0:T(8,128)(2,1)S(1)}, bf16[512,128]{1,0:T(8,128)(2,1)S(1)}, u32[]{:S(2)}, u32[]{:S(2)}) collective-permute-start(bf16[512,128]{1,0:T(8,128)(2,1)S(1)} %get-tuple-element.88), channel_id=1, source_target_pairs={{0,12},{1,13},{2,14},{3,15},{4,0},{5,1},{6,2},{7,3},{8,4},{9,5},{1... | collective-permute-start | bytes 393224 | tf_op jit(solution)/shard_map/ppermute | solution.py:262
  189.4 24.0 %collective-permute-start.39 = (bf16[512,128]{1,0:T(8,128)(2,1)}, bf16[512,128]{1,0:T(8,128)(2,1)S(1)}, u32[]{:S(2)}, u32[]{:S(2)}) collective-permute-start(bf16[512,128]{1,0:T(8,128)(2,1)} %get-tuple-element.98), channel_id=1, source_target_pairs={{0,4},{1,5},{2,6},{3,7},{4,8},{5,9},{6,10},{7,11},{8,12},{9,13},{1... | collective-permute-start | bytes 393224 | tf_op jit(solution)/shard_map/ppermute | solution.py:262
  206.1 8.6 %collective-permute-start.40 = (bf16[512,128]{1,0:T(8,128)(2,1)}, bf16[512,128]{1,0:T(8,128)(2,1)S(1)}, u32[]{:S(2)}, u32[]{:S(2)}) collective-permute-start(bf16[512,128]{1,0:T(8,128)(2,1)} %get-tuple-element.99), channel_id=1, source_target_pairs={{0,8},{1,9},{2,10},{3,11},{4,12},{5,13},{6,14},{7,15},{8,0},{9,1},... | collective-permute-start | bytes 393224 | tf_op jit(solution)/shard_map/ppermute | solution.py:262
  210.7 5.1 %collective-permute-start.41 = (bf16[512,128]{1,0:T(8,128)(2,1)S(1)}, bf16[512,128]{1,0:T(8,128)(2,1)S(1)}, u32[]{:S(2)}, u32[]{:S(2)}) collective-permute-start(bf16[512,128]{1,0:T(8,128)(2,1)S(1)} %get-tuple-element.100), channel_id=1, source_target_pairs={{0,12},{1,13},{2,14},{3,15},{4,0},{5,1},{6,2},{7,3},{8,4},{9,5},{1... | collective-permute-start | bytes 393224 | tf_op jit(solution)/shard_map/ppermute | solution.py:262
  (3 other events, 2.0 us)
where the time goes:
time: 220 us; the launch traced here: 218 us
  starting transfers between devices  100 us (45%)
  waiting for transfers between devices  82.3 us (37%)
  Pallas kernels  30.1 us (14%)
  local copies, waits for them, and re-layouts  3.73 us (2%)
    ppermute x24, starting transfers between devices, over_z(): return lax.ppermute(v, ('z', 'core'), pairs)  74.9 us
    ppermute x24, waiting for transfers between devices, over_z(): return lax.ppermute(v, ('z', 'core'), pairs)  43.3 us
    ppermute x12, waiting for transfers between devices, over_x(): return lax.ppermute(v, 'x', [(i, (i + dx) % NX) for i in range(NX)])  26 us
    pallas_call x4, Pallas kernels, products(): pl.pallas_call(functools.partial(products_kernel, parts=parts), in_specs=...  17.7 us
    ppermute x12, starting transfers between devices, over_x(): return lax.ppermute(v, 'x', [(i, (i + dx) % NX) for i in range(NX)])  15 us
    ppermute x6, waiting for transfers between devices, over_y(): return lax.ppermute(v, 'grp', [(i, (i + d) % NY) for i in range(NY)])  13 us
    ppermute x6, starting transfers between devices, over_y(): return lax.ppermute(v, 'grp', [(i, (i + d) % NY) for i in range(NY)])  10.4 us
    pallas_call x4, Pallas kernels, combine(): pl.pallas_call(combine_kernel, in_specs=[whole] * NX, out_specs=[whole] *...  6.31 us
  transfers between devices with their start and end apart: 42, of which 13 were waited for; matrix products, arithmetic and copies ran while one was open for 0% of the time, Pallas kernels for 11%

commit v1 on v0

--- a/solution.py
+++ b/solution.py
@@ -101,21 +101,14 @@
     )(place, src, owner, target, count, left, *rights)
 
 
-def first_move(dc, dz):
-    if dz % 2 == 0:
-        return 2 * dc, dz // 2
-    return (1, dz // 2) if dc == 0 else (3, (dz + 1) // 2 % HOPS)
-
-
 def combine_kernel(*refs):
     arrived, outs = refs[:NX], refs[NX:]
     step = 32
     tags = [a[PER_X * ROWS:SENT_ROWS, :].astype(jnp.float32) for a in arrived]
     for i in range(PER_X):
         tag = [jnp.broadcast_to(t[i:i + 1, :], (step, COLS)) for t in tags]
-        way, left = first_move(i // NZ, i % NZ)
-
-        def rows_of(r, carry, i=i, tag=tag, out=outs[way], start=left * SUM_ROWS):
+
+        def rows_of(r, carry, i=i, tag=tag, out=outs[i // NZ], start=i % NZ * SUM_ROWS):
             base = pl.multiple_of(r * step, step)
             sums = [jnp.zeros((step, COLS), jnp.float32) for _ in range(TARGETS)]
             for g in range(NX):
@@ -123,52 +116,78 @@
                 for t in range(TARGETS):
                     sums[t] = sums[t] + jnp.where(tag[g] == float(t), v, 0.0)
             for t in range(TARGETS):
-                out[pl.ds(start + t * ROWS + base, step), :] = sums[t].astype(jnp.bfloat16)
+                out[pl.ds(start + t * ROWS + base, step), :] = sums[t].astype(out.dtype)
             return carry
 
         lax.fori_loop(0, ROWS // step, rows_of, 0)
 
 
-def combine(arrived):
+def in_vmem(kernel, inputs, shapes):
     whole = pl.BlockSpec(memory_space=pltpu.VMEM)
     return pl.pallas_call(
-        combine_kernel,
-        in_specs=[whole] * NX,
-        out_specs=[whole] * 4,
-        out_shape=[jax.ShapeDtypeStruct((HOPS * SUM_ROWS, COLS), jnp.bfloat16)] * 4,
+        kernel,
+        in_specs=[whole] * len(inputs),
+        out_specs=[whole] * len(shapes),
+        out_shape=[jax.ShapeDtypeStruct((rows, COLS), dtype) for rows, dtype in shapes],
         compiler_params=pltpu.CompilerParams(vmem_limit_bytes=VMEM),
         cost_estimate=pl.CostEstimate(
-            flops=8 * SPOTS * ROWS * COLS, bytes_accessed=4 * 1024 * 1024, transcendentals=0),
-        name="combine",
-    )(*arrived)
-
-
-def merge_kernel(*refs):
-    parts, outs = refs[:4], refs[4:]
+            flops=8 * SPOTS * ROWS * COLS, bytes_accessed=3 * 1024 * 1024, transcendentals=0),
+    )(*inputs)
+
+
+def combine(arrived):
+    rows = NZ * SUM_ROWS
+    return in_vmem(combine_kernel, arrived, [(rows, jnp.float32), (rows, jnp.bfloat16)])
+
+
+def split_kernel(keep, swapped, even, up, down):
     step = 64
+    half = SUM_ROWS // 2
+
+    def add(out, at, start, count):
+        def rows_of(r, carry):
+            base = pl.multiple_of(r * step, step)
+            total = keep[pl.ds(start + base, step), :] + swapped[pl.ds(start + base, step), :].astype(jnp.float32)
+            out[pl.ds(at + base, step), :] = total.astype(out.dtype)
+            return carry
+
+        lax.fori_loop(0, count // step, rows_of, 0)
+
+    for dz in range(NZ):
+        if dz % 2 == 0:
+            add(even, dz // 2 * SUM_ROWS, dz * SUM_ROWS, SUM_ROWS)
+        else:
+            add(up, dz // 2 * half, dz * SUM_ROWS, half)
+            add(down, (dz + 1) // 2 % HOPS * half, dz * SUM_ROWS + half, half)
+
+
+def split(keep, swapped):
+    rows = HOPS * SUM_ROWS
+    return in_vmem(
+        split_kernel, (keep, swapped),
+        [(rows, jnp.float32), (rows // 2, jnp.bfloat16), (rows // 2, jnp.bfloat16)])
+
+
+def merge_kernel(even, up, down, *outs):
+    step = 64
+    half = SUM_ROWS // 2
     for h, out in enumerate(outs):
-
-        def rows_of(r, carry, h=h, out=out):
-            base = pl.multiple_of(r * step, step)
-            total = [p[pl.ds(h * SUM_ROWS + base, step), :].astype(jnp.float32) for p in parts]
-            out[pl.ds(base, step), :] = (total[0] + total[1] + (total[2] + total[3])).astype(jnp.bfloat16)
-            return carry
-
-        lax.fori_loop(0, SUM_ROWS // step, rows_of, 0)
+        for part, moved in enumerate((up, down)):
+
+            def rows_of(r, carry, h=h, out=out, part=part, moved=moved):
+                base = pl.multiple_of(r * step, step)
+                total = even[pl.ds(h * SUM_ROWS + part * half + base, step), :] + moved[
+                    pl.ds(h * half + base, step), :].astype(jnp.float32)
+                out[pl.ds(part * half + base, step), :] = total.astype(out.dtype)
+                return carry
+
+            lax.fori_loop(0, half // step, rows_of, 0)
 
 
 def merge(parts):
-    whole = pl.BlockSpec(memory_space=pltpu.VMEM)
-    return pl.pallas_call(
-        merge_kernel,
-        in_specs=[whole] * 4,
-        out_specs=[whole] * HOPS,
-        out_shape=[jax.ShapeDtypeStruct((SUM_ROWS, COLS), jnp.bfloat16)] * HOPS,
-        compiler_params=pltpu.CompilerParams(vmem_limit_bytes=VMEM),
-        cost_estimate=pl.CostEstimate(
-            flops=4 * HOPS * SUM_ROWS * COLS, bytes_accessed=2 * 1024 * 1024, transcendentals=0),
-        name="merge",
-    )(*parts)
+    return in_vmem(
+        merge_kernel, parts,
+        [(SUM_ROWS, jnp.float32)] + [(SUM_ROWS, jnp.bfloat16)] * (HOPS - 1))
 
 
 def block_sum(parts):
@@ -278,8 +297,10 @@
     for right in rights:
         packed = products(*slots, panels, right)
         arrived = [packed[0]] + [over_x(packed[d], d) for d in range(1, NX)]
-        keep, plus, swap, cross = combine(arrived)
-        parts = [keep, over_z(plus, 1, 0), over_z(swap, 0, 1), over_z(cross, -1, 1)]
+        keep, other = combine(arrived)
+        swapped = over_z(other, 0, 1)
+        even, up, down = split(keep, swapped)
+        parts = (even, over_z(up, 1, 0), over_z(down, -1, 0))
         merged = merge(parts)
         summed.append([merged[0]] + [over_z(merged[h], 2 * h, 0) for h in range(1, HOPS)])
     sofar = finish(piece, parent, summed[:3])

time: 220 us -> 237 us (1.077)
  the two profiles are of different devices: /device:TPU:1 before, /device:TPU:38 now
where the time goes in v1:
time: 237 us
  waiting for transfers between devices  114 us (48%)
  starting transfers between devices  83.2 us (35%)
  Pallas kernels  34.4 us (15%)
  local copies, waits for them, and re-layouts  3.53 us (1%)
    ppermute x24, starting transfers between devices, over_z(): return lax.ppermute(v, ('z', 'core'), pairs)  63.2 us
    ppermute x12, waiting for transfers between devices, over_x(): return lax.ppermute(v, 'x', [(i, (i + dx) % NX) for i in range(NX)])  56.1 us
    ppermute x6, waiting for transfers between devices, over_y(): return lax.ppermute(v, 'grp', [(i, (i + d) % NY) for i in range(NY)])  35.9 us
    ppermute x24, waiting for transfers between devices, over_z(): return lax.ppermute(v, ('z', 'core'), pairs)  22.3 us
    pallas_call x4, Pallas kernels, products(): pl.pallas_call(functools.partial(products_kernel, parts=parts), in_specs=...  19.4 us
    ppermute x12, starting transfers between devices, over_x(): return lax.ppermute(v, 'x', [(i, (i + dx) % NX) for i in range(NX)])  12.5 us
    pallas_call x12, Pallas kernels, in_vmem(): pl.pallas_call(kernel, in_specs=[whole] * len(inputs), out_specs=[whole]...  10.5 us
    ppermute x6, starting transfers between devices, over_y(): return lax.ppermute(v, 'grp', [(i, (i + d) % NY) for i in range(NY)])  7.56 us
  transfers between devices with their start and end apart: 42, of which 14 were waited for; matrix products, arithmetic and copies ran while one was open for 0% of the time, Pallas kernels for 13%

profile of v1, /device:TPU:38, one launch (start us, length us, event | category | flops | bytes accessed | tf_op | source)
XLA Modules:
  0.0 236.5 jit_solution(3939377512747759797)
XLA Ops:
  0.0 2.4 %slice.6 = bf16[4,4,64,512]{3,2,1,0:T(8,128)(2,1)} slice(bf16[4,4,128,512]{3,2,1,0:T(8,128)(2,1)} %left.7), slice={[0:4], [0:4], [0:64], [0:512]} | slice | bytes 2097152 | tf_op jit(solution)/shard_map/slice | solution.py:289
  2.5 3.0 %collective-permute-start.9 = (bf16[4,4,64,512]{3,2,1,0:T(8,128)(2,1)}, bf16[4,4,64,512]{3,2,1,0:T(8,128)(2,1)S(1)}, u32[]{:S(2)}, u32[]{:S(2)}) collective-permute-start(bf16[4,4,64,512]{3,2,1,0:T(8,128)(2,1)} %slice.6), channel_id=1, source_target_pairs={{0,192},{64,0},{128,64},{192,128},{1,193},{65,1},{129,65},{193,129... | collective-permute-start | bytes 3145736 | tf_op jit(solution)/shard_map/ppermute | solution.py:272
  5.5 1.1 slice.8
  7.1 2.7 %collective-permute-start.20 = (bf16[4,4,64,512]{3,2,1,0:T(8,128)(2,1)}, bf16[4,4,64,512]{3,2,1,0:T(8,128)(2,1)}, u32[]{:S(2)}, u32[]{:S(2)}) collective-permute-start(bf16[4,4,64,512]{3,2,1,0:T(8,128)(2,1)} %slice.8), channel_id=1, source_target_pairs={{0,192},{64,0},{128,64},{192,128},{1,193},{65,1},{129,65},{193,129... | collective-permute-start | bytes 3145736 | tf_op jit(solution)/shard_map/ppermute | solution.py:272
  10.5 4.4 %products.4 = (bf16[2064,128]{1,0:T(8,128)(2,1)S(1)}, bf16[2064,128]{1,0:T(8,128)(2,1)S(1)}, bf16[2064,128]{1,0:T(8,128)(2,1)S(1)}, bf16[2064,128]{1,0:T(8,128)(2,1)S(1)}) custom-call(s32[3]{0:T(128)S(1)} %pad_add_fusion.place, s32[40]{0:T(128)S(1)} %bitcast.6, s32[40]{0:T(128)S(1)} %bitcast.10, s32[40]{0:T(128)S(1)} %copy-done.4, s32[1]{0:T(128)S(6)} %copy.9.count, ...), custom_call_target="tpu_custom_call" | custom-call | flops 671088640 | bytes 6291456 | tf_op jit(solution)/shard_map/products/pallas_call | solution.py:87
  15.5 13.8 %collective-permute-done.9.rest_0_ = bf16[4,4,64,512]{3,2,1,0:T(8,128)(2,1)S(1)} collective-permute-done((bf16[4,4,64,512]{3,2,1,0:T(8,128)(2,1)}, bf16[4,4,64,512]{3,2,1,0:T(8,128)(2,1)S(1)}, u32[]{:S(2)}, u32[]{:S(2)}) %collective-permute-start.9) | collective-permute-done | bytes 1048608 | tf_op jit(solution)/shard_map/ppermute | solution.py:272
  29.3 1.4 collective-permute-start.1
  30.7 2.3 collective-permute-done.10.rest_1_
  33.0 1.3 collective-permute-start.31
  34.3 19.8 %collective-permute-done.21.rest_1_ = bf16[4,4,64,512]{3,2,1,0:T(8,128)(2,1)} collective-permute-done((bf16[4,4,64,512]{3,2,1,0:T(8,128)(2,1)}, bf16[4,4,64,512]{3,2,1,0:T(8,128)(2,1)}, u32[]{:S(2)}, u32[]{:S(2)}) %collective-permute-start.21) | collective-permute-done | bytes 1048608 | tf_op jit(solution)/shard_map/ppermute | solution.py:272
  54.1 5.1 %products.5 = (bf16[2064,128]{1,0:T(8,128)(2,1)S(1)}, bf16[2064,128]{1,0:T(8,128)(2,1)S(1)}, bf16[2064,128]{1,0:T(8,128)(2,1)S(1)}, bf16[2064,128]{1,0:T(8,128)(2,1)S(1)}) custom-call(s32[3]{0:T(128)S(1)} %pad_add_fusion.place, s32[40]{0:T(128)S(1)} %bitcast.7, s32[40]{0:T(128)S(1)} %bitcast.11, s32[40]{0:T(128)S(1)} %copy-done.4, s32[1]{0:T(128)S(6)} %copy.9.count, ...), custom_call_target="tpu_custom_call" | custom-call | flops 671088640 | bytes 6291456 | tf_op jit(solution)/shard_map/products/pallas_call | solution.py:87
  60.1 2.4 %collective-permute-start.11 = (bf16[2064,128]{1,0:T(8,128)(2,1)S(1)}, bf16[2064,128]{1,0:T(8,128)(2,1)S(1)}, u32[]{:S(2)}, u32[]{:S(2)}) collective-permute-start(bf16[2064,128]{1,0:T(8,128)(2,1)S(1)} %get-tuple-element.71), channel_id=1, source_target_pairs={{0,16},{16,32},{32,48},{48,0},{1,17},{17,33},{33,49},{49,1},{2,18}... | collective-permute-start | bytes 1585160 | tf_op jit(solution)/shard_map/ppermute | solution.py:276
  62.7 5.4 %products.6 = (bf16[2064,128]{1,0:T(8,128)(2,1)S(1)}, bf16[2064,128]{1,0:T(8,128)(2,1)S(1)}, bf16[2064,128]{1,0:T(8,128)(2,1)S(1)}, bf16[2064,128]{1,0:T(8,128)(2,1)S(1)}) custom-call(s32[3]{0:T(128)S(1)} %pad_add_fusion.place, s32[40]{0:T(128)S(1)} %bitcast.8, s32[40]{0:T(128)S(1)} %bitcast.12, s32[40]{0:T(128)S(1)} %copy-done.4, s32[1]{0:T(128)S(6)} %copy.9.count, ...), custom_call_target="tpu_custom_call" | custom-call | flops 671088640 | bytes 6291456 | tf_op jit(solution)/shard_map/products/pallas_call | solution.py:87
  68.2 17.5 %collective-permute-done.2.refs_3_ = bf16[2064,128]{1,0:T(8,128)(2,1)S(1)} collective-permute-done((bf16[2064,128]{1,0:T(8,128)(2,1)S(1)}, bf16[2064,128]{1,0:T(8,128)(2,1)S(1)}, u32[]{:S(2)}, u32[]{:S(2)}) %collective-permute-start.2) | collective-permute-done | bytes 528416 | tf_op jit(solution)/shard_map/ppermute | solution.py:276
  85.7 3.2 %collective-permute-start.22 = (bf16[2064,128]{1,0:T(8,128)(2,1)S(1)}, bf16[2064,128]{1,0:T(8,128)(2,1)S(1)}, u32[]{:S(2)}, u32[]{:S(2)}) collective-permute-start(bf16[2064,128]{1,0:T(8,128)(2,1)S(1)} %get-tuple-element.84), channel_id=1, source_target_pairs={{0,16},{16,32},{32,48},{48,0},{1,17},{17,33},{33,49},{49,1},{2,18}... | collective-permute-start | bytes 1585160 | tf_op jit(solution)/shard_map/ppermute | solution.py:276
  89.8 4.4 %products.7 = (bf16[2064,128]{1,0:T(8,128)(2,1)S(1)}, bf16[2064,128]{1,0:T(8,128)(2,1)S(1)}, bf16[2064,128]{1,0:T(8,128)(2,1)S(1)}, bf16[2064,128]{1,0:T(8,128)(2,1)S(1)}) custom-call(s32[3]{0:T(128)S(1)} %pad_add_fusion.place, s32[40]{0:T(128)S(1)} %bitcast.9, s32[40]{0:T(128)S(1)} %bitcast.13, s32[40]{0:T(128)S(1)} %copy-done.4, s32[1]{0:T(128)S(6)} %copy.9.count, ...), custom_call_target="tpu_custom_call" | custom-call | flops 671088640 | bytes 6291456 | tf_op jit(solution)/shard_map/products/pallas_call | solution.py:87
  94.3 2.6 %collective-permute-start.33 = (bf16[2064,128]{1,0:T(8,128)(2,1)S(1)}, bf16[2064,128]{1,0:T(8,128)(2,1)S(1)}, u32[]{:S(2)}, u32[]{:S(2)}) collective-permute-start(bf16[2064,128]{1,0:T(8,128)(2,1)S(1)} %get-tuple-element.97), channel_id=1, source_target_pairs={{0,16},{16,32},{32,48},{48,0},{1,17},{17,33},{33,49},{49,1},{2,18}... | collective-permute-start | bytes 1585160 | tf_op jit(solution)/shard_map/ppermute | solution.py:276
  96.9 16.1 %collective-permute-done.13.refs_3_ = bf16[2064,128]{1,0:T(8,128)(2,1)S(1)} collective-permute-done((bf16[2064,128]{1,0:T(8,128)(2,1)S(1)}, bf16[2064,128]{1,0:T(8,128)(2,1)S(1)}, u32[]{:S(2)}, u32[]{:S(2)}) %collective-permute-start.13) | collective-permute-done | bytes 528416 | tf_op jit(solution)/shard_map/ppermute | solution.py:276
  113.2 1.5 shard_map.64
  114.9 1.5 shard_map.67
  116.4 19.0 %collective-permute-done.24.refs_3_ = bf16[2064,128]{1,0:T(8,128)(2,1)S(1)} collective-permute-done((bf16[2064,128]{1,0:T(8,128)(2,1)S(1)}, bf16[2064,128]{1,0:T(8,128)(2,1)S(1)}, u32[]{:S(2)}, u32[]{:S(2)}) %collective-permute-start.24) | collective-permute-done | bytes 528416 | tf_op jit(solution)/shard_map/ppermute | solution.py:276
  135.4 1.5 shard_map.70
  137.6 3.5 %collective-permute-done.35.refs_3_ = bf16[2064,128]{1,0:T(8,128)(2,1)S(1)} collective-permute-done((bf16[2064,128]{1,0:T(8,128)(2,1)S(1)}, bf16[2064,128]{1,0:T(8,128)(2,1)S(1)}, u32[]{:S(2)}, u32[]{:S(2)}) %collective-permute-start.35) | collective-permute-done | bytes 528416 | tf_op jit(solution)/shard_map/ppermute | solution.py:276
  141.1 1.5 shard_map.73
  143.2 2.0 collective-permute-start.4
  145.8 2.0 collective-permute-start.15
  147.8 2.2 collective-permute-start.16
  150.5 1.9 collective-permute-done.4.up
  152.5 1.9 collective-permute-start.26
  154.4 2.0 collective-permute-start.27
  156.7 3.8 %collective-permute-start.6 = (bf16[512,128]{1,0:T(8,128)(2,1)S(1)}, bf16[512,128]{1,0:T(8,128)(2,1)S(1)}, u32[]{:S(2)}, u32[]{:S(2)}) collective-permute-start(bf16[512,128]{1,0:T(8,128)(2,1)S(1)} %get-tuple-element.67), channel_id=1, source_target_pairs={{0,4},{1,5},{2,6},{3,7},{4,8},{5,9},{6,10},{7,11},{8,12},{9,13},{1... | collective-permute-start | bytes 393224 | tf_op jit(solution)/shard_map/ppermute | solution.py:281
  160.9 3.5 %collective-permute-start.37 = (bf16[1024,128]{1,0:T(8,128)(2,1)S(1)}, bf16[1024,128]{1,0:T(8,128)(2,1)S(1)}, u32[]{:S(2)}, u32[]{:S(2)}) collective-permute-start(bf16[1024,128]{1,0:T(8,128)(2,1)S(1)} %get-tuple-element.103), channel_id=1, source_target_pairs={{0,2},{1,3},{2,4},{3,5},{4,6},{5,7},{6,8},{7,9},{8,10},{9,11},{10,... | collective-permute-start | bytes 786440 | tf_op jit(solution)/shard_map/ppermute | solution.py:281
  164.7 8.0 %collective-permute-done.6.refs_1_ = bf16[512,128]{1,0:T(8,128)(2,1)S(1)} collective-permute-done((bf16[512,128]{1,0:T(8,128)(2,1)S(1)}, bf16[512,128]{1,0:T(8,128)(2,1)S(1)}, u32[]{:S(2)}, u32[]{:S(2)}) %collective-permute-start.6) | collective-permute-done | bytes 131104 | tf_op jit(solution)/shard_map/ppermute | solution.py:281
  172.7 4.6 %collective-permute-start.7 = (bf16[512,128]{1,0:T(8,128)(2,1)S(1)}, bf16[512,128]{1,0:T(8,128)(2,1)S(1)}, u32[]{:S(2)}, u32[]{:S(2)}) collective-permute-start(bf16[512,128]{1,0:T(8,128)(2,1)S(1)} %get-tuple-element.68), channel_id=1, source_target_pairs={{0,8},{1,9},{2,10},{3,11},{4,12},{5,13},{6,14},{7,15},{8,0},{9,1},... | collective-permute-start | bytes 393224 | tf_op jit(solution)/shard_map/ppermute | solution.py:281
  177.3 2.9 %collective-permute-start.17 = (bf16[512,128]{1,0:T(8,128)(2,1)S(1)}, bf16[512,128]{1,0:T(8,128)(2,1)S(1)}, u32[]{:S(2)}, u32[]{:S(2)}) collective-permute-start(bf16[512,128]{1,0:T(8,128)(2,1)S(1)} %get-tuple-element.80), channel_id=1, source_target_pairs={{0,4},{1,5},{2,6},{3,7},{4,8},{5,9},{6,10},{7,11},{8,12},{9,13},{1... | collective-permute-start | bytes 393224 | tf_op jit(solution)/shard_map/ppermute | solution.py:281
  181.2 4.2 %collective-permute-done.7.refs_2_ = bf16[512,128]{1,0:T(8,128)(2,1)S(1)} collective-permute-done((bf16[512,128]{1,0:T(8,128)(2,1)S(1)}, bf16[512,128]{1,0:T(8,128)(2,1)S(1)}, u32[]{:S(2)}, u32[]{:S(2)}) %collective-permute-start.7) | collective-permute-done | bytes 131104 | tf_op jit(solution)/shard_map/ppermute | solution.py:281
  185.3 5.0 %collective-permute-start.18 = (bf16[512,128]{1,0:T(8,128)(2,1)S(1)}, bf16[512,128]{1,0:T(8,128)(2,1)S(1)}, u32[]{:S(2)}, u32[]{:S(2)}) collective-permute-start(bf16[512,128]{1,0:T(8,128)(2,1)S(1)} %get-tuple-element.81), channel_id=1, source_target_pairs={{0,8},{1,9},{2,10},{3,11},{4,12},{5,13},{6,14},{7,15},{8,0},{9,1},... | collective-permute-start | bytes 393224 | tf_op jit(solution)/shard_map/ppermute | solution.py:281
  190.3 1.7 collective-permute-done.17.refs_5_
  192.0 19.7 %collective-permute-start.28 = (bf16[512,128]{1,0:T(8,128)(2,1)S(1)}, bf16[512,128]{1,0:T(8,128)(2,1)S(1)}, u32[]{:S(2)}, u32[]{:S(2)}) collective-permute-start(bf16[512,128]{1,0:T(8,128)(2,1)S(1)} %get-tuple-element.93), channel_id=1, source_target_pairs={{0,4},{1,5},{2,6},{3,7},{4,8},{5,9},{6,10},{7,11},{8,12},{9,13},{1... | collective-permute-start | bytes 393224 | tf_op jit(solution)/shard_map/ppermute | solution.py:281
  211.7 4.3 %collective-permute-start.29 = (bf16[512,128]{1,0:T(8,128)(2,1)}, bf16[512,128]{1,0:T(8,128)(2,1)S(1)}, u32[]{:S(2)}, u32[]{:S(2)}) collective-permute-start(bf16[512,128]{1,0:T(8,128)(2,1)} %get-tuple-element.94), channel_id=1, source_target_pairs={{0,8},{1,9},{2,10},{3,11},{4,12},{5,13},{6,14},{7,15},{8,0},{9,1},... | collective-permute-start | bytes 393224 | tf_op jit(solution)/shard_map/ppermute | solution.py:281
  216.0 4.1 %collective-permute-start.30 = (bf16[512,128]{1,0:T(8,128)(2,1)}, bf16[512,128]{1,0:T(8,128)(2,1)S(1)}, u32[]{:S(2)}, u32[]{:S(2)}) collective-permute-start(bf16[512,128]{1,0:T(8,128)(2,1)} %get-tuple-element.95), channel_id=1, source_target_pairs={{0,12},{1,13},{2,14},{3,15},{4,0},{5,1},{6,2},{7,3},{8,4},{9,5},{1... | collective-permute-start | bytes 393224 | tf_op jit(solution)/shard_map/ppermute | solution.py:281
  221.2 2.4 collective-permute-start.40
  223.6 1.9 collective-permute-start.41
  225.4 1.8 finish.1.sofar
  227.3 1.2 collective-permute-done.39.refs_1_
  228.5 3.4 %collective-permute-done.40.refs_2_ = bf16[512,128]{1,0:T(8,128)(2,1)S(1)} collective-permute-done((bf16[512,128]{1,0:T(8,128)(2,1)}, bf16[512,128]{1,0:T(8,128)(2,1)S(1)}, u32[]{:S(2)}, u32[]{:S(2)}) %collective-permute-start.40) | collective-permute-done | bytes 131104 | tf_op jit(solution)/shard_map/ppermute | solution.py:281
  231.9 1.8 collective-permute-done.41.refs_3_
  233.7 2.6 %finish_last.1 = f32[4,128,512]{2,1,0:T(8,128)} custom-call(s32[1]{0:T(128)} %bitcast.piece, f32[4,128,512]{2,1,0:T(8,128)} %finish.1.sofar, f32[512,128]{1,0:T(8,128)S(1)} %get-tuple-element.105.refs_0_, bf16[512,128]{1,0:T(8,128)(2,1)S(1)} %collective-permute-done.39.refs_1_, ...), custom_call_target="tpu_custom_call", output_to_operand_aliasing={{}: (1, {})} | custom-call | flops 655360 | bytes 2097152 | tf_op jit(solution)/shard_map/finish_last/pallas_call | solution.py:254
  (67 shorter events, 8.9 us)
Async XLA Ops:
  0.0 5.5 %copy-start = (bf16[4,4,128,512]{3,2,1,0:T(8,128)(2,1)S(1)}, bf16[4,4,128,512]{3,2,1,0:T(8,128)(2,1)}, u32[]{:S(2)}) copy-start(bf16[4,4,128,512]{3,2,1,0:T(8,128)(2,1)} %left.7) | copy-start | bytes 6291460
  0.0 10.5 %copy-start.2 = (s32[1,40]{1,0:T(1,128)S(1)}, s32[1,40]{1,0:T(1,128)}, u32[]{:S(2)}) copy-start(s32[1,40]{1,0:T(1,128)} %param.8) | copy-start | bytes 484
  0.0 10.5 %copy-start.3 = (s32[40,1]{0,1:T(1,128)S(1)}, s32[40,1]{0,1:T(1,128)}, u32[]{:S(2)}) copy-start(s32[40,1]{0,1:T(1,128)} %param.9) | copy-start | bytes 484
  0.0 10.5 %copy-start.4 = (s32[40]{0:T(128)S(1)}, s32[40]{0:T(128)}, u32[]{:S(2)}) copy-start(s32[40]{0:T(128)} %target.7) | copy-start | bytes 484
  2.5 26.9 %collective-permute-start.9 = (bf16[4,4,64,512]{3,2,1,0:T(8,128)(2,1)}, bf16[4,4,64,512]{3,2,1,0:T(8,128)(2,1)S(1)}, u32[]{:S(2)}, u32[]{:S(2)}) collective-permute-start(bf16[4,4,64,512]{3,2,1,0:T(8,128)(2,1)} %slice.6), channel_id=1, source_target_pairs={{0,192},{64,0},{128,64},{192,128},{1,193},{65,1},{129,65},{193,129... | collective-permute-start | bytes 3145736 | tf_op jit(solution)/shard_map/ppermute | solution.py:272
  5.5 27.6 %collective-permute-start.10 = (bf16[4,4,64,512]{3,2,1,0:T(8,128)(2,1)}, bf16[4,4,64,512]{3,2,1,0:T(8,128)(2,1)}, u32[]{:S(2)}, u32[]{:S(2)}) collective-permute-start(bf16[4,4,64,512]{3,2,1,0:T(8,128)(2,1)} %slice.6), channel_id=1, source_target_pairs={{0,64},{64,128},{128,192},{192,0},{1,65},{65,129},{129,193},{193,1... | collective-permute-start | bytes 3145736 | tf_op jit(solution)/shard_map/ppermute | solution.py:272
  6.6 47.5 %collective-permute-start.21 = (bf16[4,4,64,512]{3,2,1,0:T(8,128)(2,1)}, bf16[4,4,64,512]{3,2,1,0:T(8,128)(2,1)}, u32[]{:S(2)}, u32[]{:S(2)}) collective-permute-start(bf16[4,4,64,512]{3,2,1,0:T(8,128)(2,1)} %slice.8), channel_id=1, source_target_pairs={{0,64},{64,128},{128,192},{192,0},{1,65},{65,129},{129,193},{193,1... | collective-permute-start | bytes 3145736 | tf_op jit(solution)/shard_map/ppermute | solution.py:272
  7.1 55.4 %collective-permute-start.20 = (bf16[4,4,64,512]{3,2,1,0:T(8,128)(2,1)}, bf16[4,4,64,512]{3,2,1,0:T(8,128)(2,1)}, u32[]{:S(2)}, u32[]{:S(2)}) collective-permute-start(bf16[4,4,64,512]{3,2,1,0:T(8,128)(2,1)} %slice.8), channel_id=1, source_target_pairs={{0,192},{64,0},{128,64},{192,128},{1,193},{65,1},{129,65},{193,129... | collective-permute-start | bytes 3145736 | tf_op jit(solution)/shard_map/ppermute | solution.py:272
  15.0 44.2 %collective-permute-start = (bf16[2064,128]{1,0:T(8,128)(2,1)S(1)}, bf16[2064,128]{1,0:T(8,128)(2,1)S(1)}, u32[]{:S(2)}, u32[]{:S(2)}) collective-permute-start(bf16[2064,128]{1,0:T(8,128)(2,1)S(1)} %get-tuple-element.58), channel_id=1, source_target_pairs={{0,16},{16,32},{32,48},{48,0},{1,17},{17,33},{33,49},{49,1},{2,18}... | collective-permute-start | bytes 1585160 | tf_op jit(solution)/shard_map/ppermute | solution.py:276
  29.3 30.8 %collective-permute-start.1 = (bf16[2064,128]{1,0:T(8,128)(2,1)S(1)}, bf16[2064,128]{1,0:T(8,128)(2,1)S(1)}, u32[]{:S(2)}, u32[]{:S(2)}) collective-permute-start(bf16[2064,128]{1,0:T(8,128)(2,1)S(1)} %get-tuple-element.59), channel_id=1, source_target_pairs={{0,32},{16,48},{32,0},{48,16},{1,33},{17,49},{33,1},{49,17},{2,34}... | collective-permute-start | bytes 1585160 | tf_op jit(solution)/shard_map/ppermute | solution.py:276
  33.0 55.9 %collective-permute-start.31 = (bf16[4,4,64,512]{3,2,1,0:T(8,128)(2,1)S(1)}, bf16[4,4,64,512]{3,2,1,0:T(8,128)(2,1)S(1)}, u32[]{:S(2)}, u32[]{:S(2)}) collective-permute-start(bf16[4,4,64,512]{3,2,1,0:T(8,128)(2,1)S(1)} %collective-permute-done.9.rest_0_), channel_id=1, source_target_pairs={{0,192},{64,0},{128,64},{192,128},{1,193},{65,1},{129,65},{193,129... | collective-permute-start | bytes 3145736 | tf_op jit(solution)/shard_map/ppermute | solution.py:272
  54.1 34.8 %collective-permute-start.32 = (bf16[4,4,64,512]{3,2,1,0:T(8,128)(2,1)}, bf16[4,4,64,512]{3,2,1,0:T(8,128)(2,1)S(1)}, u32[]{:S(2)}, u32[]{:S(2)}) collective-permute-start(bf16[4,4,64,512]{3,2,1,0:T(8,128)(2,1)} %collective-permute-done.21.rest_1_), channel_id=1, source_target_pairs={{0,64},{64,128},{128,192},{192,0},{1,65},{65,129},{129,193},{193,1... | collective-permute-start | bytes 3145736 | tf_op jit(solution)/shard_map/ppermute | solution.py:272
  59.2 26.4 %collective-permute-start.2 = (bf16[2064,128]{1,0:T(8,128)(2,1)S(1)}, bf16[2064,128]{1,0:T(8,128)(2,1)S(1)}, u32[]{:S(2)}, u32[]{:S(2)}) collective-permute-start(bf16[2064,128]{1,0:T(8,128)(2,1)S(1)} %get-tuple-element.60), channel_id=1, source_target_pairs={{0,48},{16,0},{32,16},{48,32},{1,49},{17,1},{33,17},{49,33},{2,50}... | collective-permute-start | bytes 1585160 | tf_op jit(solution)/shard_map/ppermute | solution.py:276
  60.1 25.5 %collective-permute-start.11 = (bf16[2064,128]{1,0:T(8,128)(2,1)S(1)}, bf16[2064,128]{1,0:T(8,128)(2,1)S(1)}, u32[]{:S(2)}, u32[]{:S(2)}) collective-permute-start(bf16[2064,128]{1,0:T(8,128)(2,1)S(1)} %get-tuple-element.71), channel_id=1, source_target_pairs={{0,16},{16,32},{32,48},{48,0},{1,17},{17,33},{33,49},{49,1},{2,18}... | collective-permute-start | bytes 1585160 | tf_op jit(solution)/shard_map/ppermute | solution.py:276
  62.5 31.8 %collective-permute-start.12 = (bf16[2064,128]{1,0:T(8,128)(2,1)S(1)}, bf16[2064,128]{1,0:T(8,128)(2,1)S(1)}, u32[]{:S(2)}, u32[]{:S(2)}) collective-permute-start(bf16[2064,128]{1,0:T(8,128)(2,1)S(1)} %get-tuple-element.72), channel_id=1, source_target_pairs={{0,32},{16,48},{32,0},{48,16},{1,33},{17,49},{33,1},{49,17},{2,34}... | collective-permute-start | bytes 1585160 | tf_op jit(solution)/shard_map/ppermute | solution.py:276
  85.6 27.4 %collective-permute-start.13 = (bf16[2064,128]{1,0:T(8,128)(2,1)S(1)}, bf16[2064,128]{1,0:T(8,128)(2,1)S(1)}, u32[]{:S(2)}, u32[]{:S(2)}) collective-permute-start(bf16[2064,128]{1,0:T(8,128)(2,1)S(1)} %get-tuple-element.73), channel_id=1, source_target_pairs={{0,48},{16,0},{32,16},{48,32},{1,49},{17,1},{33,17},{49,33},{2,50}... | collective-permute-start | bytes 1585160 | tf_op jit(solution)/shard_map/ppermute | solution.py:276
  85.7 27.4 %collective-permute-start.22 = (bf16[2064,128]{1,0:T(8,128)(2,1)S(1)}, bf16[2064,128]{1,0:T(8,128)(2,1)S(1)}, u32[]{:S(2)}, u32[]{:S(2)}) collective-permute-start(bf16[2064,128]{1,0:T(8,128)(2,1)S(1)} %get-tuple-element.84), channel_id=1, source_target_pairs={{0,16},{16,32},{32,48},{48,0},{1,17},{17,33},{33,49},{49,1},{2,18}... | collective-permute-start | bytes 1585160 | tf_op jit(solution)/shard_map/ppermute | solution.py:276
  88.9 25.9 %collective-permute-start.23 = (bf16[2064,128]{1,0:T(8,128)(2,1)S(1)}, bf16[2064,128]{1,0:T(8,128)(2,1)S(1)}, u32[]{:S(2)}, u32[]{:S(2)}) collective-permute-start(bf16[2064,128]{1,0:T(8,128)(2,1)S(1)} %get-tuple-element.85), channel_id=1, source_target_pairs={{0,32},{16,48},{32,0},{48,16},{1,33},{17,49},{33,1},{49,17},{2,34}... | collective-permute-start | bytes 1585160 | tf_op jit(solution)/shard_map/ppermute | solution.py:276
  88.9 46.5 %collective-permute-start.24 = (bf16[2064,128]{1,0:T(8,128)(2,1)S(1)}, bf16[2064,128]{1,0:T(8,128)(2,1)S(1)}, u32[]{:S(2)}, u32[]{:S(2)}) collective-permute-start(bf16[2064,128]{1,0:T(8,128)(2,1)S(1)} %get-tuple-element.86), channel_id=1, source_target_pairs={{0,48},{16,0},{32,16},{48,32},{1,49},{17,1},{33,17},{49,33},{2,50}... | collective-permute-start | bytes 1585160 | tf_op jit(solution)/shard_map/ppermute | solution.py:276
  94.3 42.6 %collective-permute-start.33 = (bf16[2064,128]{1,0:T(8,128)(2,1)S(1)}, bf16[2064,128]{1,0:T(8,128)(2,1)S(1)}, u32[]{:S(2)}, u32[]{:S(2)}) collective-permute-start(bf16[2064,128]{1,0:T(8,128)(2,1)S(1)} %get-tuple-element.97), channel_id=1, source_target_pairs={{0,16},{16,32},{32,48},{48,0},{1,17},{17,33},{33,49},{49,1},{2,18}... | collective-permute-start | bytes 1585160 | tf_op jit(solution)/shard_map/ppermute | solution.py:276
  113.0 24.5 %collective-permute-start.34 = (bf16[2064,128]{1,0:T(8,128)(2,1)S(1)}, bf16[2064,128]{1,0:T(8,128)(2,1)S(1)}, u32[]{:S(2)}, u32[]{:S(2)}) collective-permute-start(bf16[2064,128]{1,0:T(8,128)(2,1)S(1)} %get-tuple-element.98), channel_id=1, source_target_pairs={{0,32},{16,48},{32,0},{48,16},{1,33},{17,49},{33,1},{49,17},{2,34}... | collective-permute-start | bytes 1585160 | tf_op jit(solution)/shard_map/ppermute | solution.py:276
  113.0 28.0 %collective-permute-start.35 = (bf16[2064,128]{1,0:T(8,128)(2,1)S(1)}, bf16[2064,128]{1,0:T(8,128)(2,1)S(1)}, u32[]{:S(2)}, u32[]{:S(2)}) collective-permute-start(bf16[2064,128]{1,0:T(8,128)(2,1)S(1)} %get-tuple-element.99), channel_id=1, source_target_pairs={{0,48},{16,0},{32,16},{48,32},{1,49},{17,1},{33,17},{49,33},{2,50}... | collective-permute-start | bytes 1585160 | tf_op jit(solution)/shard_map/ppermute | solution.py:276
  114.8 27.9 %collective-permute-start.3 = (bf16[4096,128]{1,0:T(8,128)(2,1)S(1)}, bf16[4096,128]{1,0:T(8,128)(2,1)S(1)}, u32[]{:S(2)}, u32[]{:S(2)}) collective-permute-start(bf16[4096,128]{1,0:T(8,128)(2,1)S(1)} %get-tuple-element.62), channel_id=1, source_target_pairs={{0,1},{1,0},{2,3},{3,2},{4,5},{5,4},{6,7},{7,6},{8,9},{9,8},{10,11... | collective-permute-start | bytes 3145736 | tf_op jit(solution)/shard_map/ppermute | solution.py:281
  135.4 9.9 %collective-permute-start.14 = (bf16[4096,128]{1,0:T(8,128)(2,1)S(1)}, bf16[4096,128]{1,0:T(8,128)(2,1)S(1)}, u32[]{:S(2)}, u32[]{:S(2)}) collective-permute-start(bf16[4096,128]{1,0:T(8,128)(2,1)S(1)} %get-tuple-element.75), channel_id=1, source_target_pairs={{0,1},{1,0},{2,3},{3,2},{4,5},{5,4},{6,7},{7,6},{8,9},{9,8},{10,11... | collective-permute-start | bytes 3145736 | tf_op jit(solution)/shard_map/ppermute | solution.py:281
  137.0 10.9 %collective-permute-start.25 = (bf16[4096,128]{1,0:T(8,128)(2,1)S(1)}, bf16[4096,128]{1,0:T(8,128)(2,1)S(1)}, u32[]{:S(2)}, u32[]{:S(2)}) collective-permute-start(bf16[4096,128]{1,0:T(8,128)(2,1)S(1)} %get-tuple-element.88), channel_id=1, source_target_pairs={{0,1},{1,0},{2,3},{3,2},{4,5},{5,4},{6,7},{7,6},{8,9},{9,8},{10,11... | collective-permute-start | bytes 3145736 | tf_op jit(solution)/shard_map/ppermute | solution.py:281
  142.6 14.1 %collective-permute-start.36 = (bf16[4096,128]{1,0:T(8,128)(2,1)S(1)}, bf16[4096,128]{1,0:T(8,128)(2,1)S(1)}, u32[]{:S(2)}, u32[]{:S(2)}) collective-permute-start(bf16[4096,128]{1,0:T(8,128)(2,1)S(1)} %get-tuple-element.101), channel_id=1, source_target_pairs={{0,1},{1,0},{2,3},{3,2},{4,5},{5,4},{6,7},{7,6},{8,9},{9,8},{10,11... | collective-permute-start | bytes 3145736 | tf_op jit(solution)/shard_map/ppermute | solution.py:281
  143.2 9.3 %collective-permute-start.4 = (bf16[1024,128]{1,0:T(8,128)(2,1)S(1)}, bf16[1024,128]{1,0:T(8,128)(2,1)S(1)}, u32[]{:S(2)}, u32[]{:S(2)}) collective-permute-start(bf16[1024,128]{1,0:T(8,128)(2,1)S(1)} %get-tuple-element.64), channel_id=1, source_target_pairs={{0,2},{1,3},{2,4},{3,5},{4,6},{5,7},{6,8},{7,9},{8,10},{9,11},{10,... | collective-permute-start | bytes 786440 | tf_op jit(solution)/shard_map/ppermute | solution.py:281
  145.2 9.2 %collective-permute-start.5 = (bf16[1024,128]{1,0:T(8,128)(2,1)S(1)}, bf16[1024,128]{1,0:T(8,128)(2,1)S(1)}, u32[]{:S(2)}, u32[]{:S(2)}) collective-permute-start(bf16[1024,128]{1,0:T(8,128)(2,1)S(1)} %get-tuple-element.65), channel_id=1, source_target_pairs={{0,14},{1,15},{2,0},{3,1},{4,2},{5,3},{6,4},{7,5},{8,6},{9,7},{10,... | collective-permute-start | bytes 786440 | tf_op jit(solution)/shard_map/ppermute | solution.py:281
  145.8 15.1 %collective-permute-start.15 = (bf16[1024,128]{1,0:T(8,128)(2,1)S(1)}, bf16[1024,128]{1,0:T(8,128)(2,1)S(1)}, u32[]{:S(2)}, u32[]{:S(2)}) collective-permute-start(bf16[1024,128]{1,0:T(8,128)(2,1)S(1)} %get-tuple-element.77), channel_id=1, source_target_pairs={{0,2},{1,3},{2,4},{3,5},{4,6},{5,7},{6,8},{7,9},{8,10},{9,11},{10,... | collective-permute-start | bytes 786440 | tf_op jit(solution)/shard_map/ppermute | solution.py:281
  147.8 16.7 %collective-permute-start.16 = (bf16[1024,128]{1,0:T(8,128)(2,1)S(1)}, bf16[1024,128]{1,0:T(8,128)(2,1)S(1)}, u32[]{:S(2)}, u32[]{:S(2)}) collective-permute-start(bf16[1024,128]{1,0:T(8,128)(2,1)S(1)} %get-tuple-element.78), channel_id=1, source_target_pairs={{0,14},{1,15},{2,0},{3,1},{4,2},{5,3},{6,4},{7,5},{8,6},{9,7},{10,... | collective-permute-start | bytes 786440 | tf_op jit(solution)/shard_map/ppermute | solution.py:281
  152.5 24.8 %collective-permute-start.26 = (bf16[1024,128]{1,0:T(8,128)(2,1)S(1)}, bf16[1024,128]{1,0:T(8,128)(2,1)S(1)}, u32[]{:S(2)}, u32[]{:S(2)}) collective-permute-start(bf16[1024,128]{1,0:T(8,128)(2,1)S(1)} %get-tuple-element.90), channel_id=1, source_target_pairs={{0,2},{1,3},{2,4},{3,5},{4,6},{5,7},{6,8},{7,9},{8,10},{9,11},{10,... | collective-permute-start | bytes 786440 | tf_op jit(solution)/shard_map/ppermute | solution.py:281
  154.4 22.9 %collective-permute-start.27 = (bf16[1024,128]{1,0:T(8,128)(2,1)S(1)}, bf16[1024,128]{1,0:T(8,128)(2,1)S(1)}, u32[]{:S(2)}, u32[]{:S(2)}) collective-permute-start(bf16[1024,128]{1,0:T(8,128)(2,1)S(1)} %get-tuple-element.91), channel_id=1, source_target_pairs={{0,14},{1,15},{2,0},{3,1},{4,2},{5,3},{6,4},{7,5},{8,6},{9,7},{10,... | collective-permute-start | bytes 786440 | tf_op jit(solution)/shard_map/ppermute | solution.py:281
  156.7 16.0 %collective-permute-start.6 = (bf16[512,128]{1,0:T(8,128)(2,1)S(1)}, bf16[512,128]{1,0:T(8,128)(2,1)S(1)}, u32[]{:S(2)}, u32[]{:S(2)}) collective-permute-start(bf16[512,128]{1,0:T(8,128)(2,1)S(1)} %get-tuple-element.67), channel_id=1, source_target_pairs={{0,4},{1,5},{2,6},{3,7},{4,8},{5,9},{6,10},{7,11},{8,12},{9,13},{1... | collective-permute-start | bytes 393224 | tf_op jit(solution)/shard_map/ppermute | solution.py:281
  160.9 50.8 %collective-permute-start.37 = (bf16[1024,128]{1,0:T(8,128)(2,1)S(1)}, bf16[1024,128]{1,0:T(8,128)(2,1)S(1)}, u32[]{:S(2)}, u32[]{:S(2)}) collective-permute-start(bf16[1024,128]{1,0:T(8,128)(2,1)S(1)} %get-tuple-element.103), channel_id=1, source_target_pairs={{0,2},{1,3},{2,4},{3,5},{4,6},{5,7},{6,8},{7,9},{8,10},{9,11},{10,... | collective-permute-start | bytes 786440 | tf_op jit(solution)/shard_map/ppermute | solution.py:281
  164.5 51.6 %collective-permute-start.38 = (bf16[1024,128]{1,0:T(8,128)(2,1)S(1)}, bf16[1024,128]{1,0:T(8,128)(2,1)S(1)}, u32[]{:S(2)}, u32[]{:S(2)}) collective-permute-start(bf16[1024,128]{1,0:T(8,128)(2,1)S(1)} %get-tuple-element.104), channel_id=1, source_target_pairs={{0,14},{1,15},{2,0},{3,1},{4,2},{5,3},{6,4},{7,5},{8,6},{9,7},{10,... | collective-permute-start | bytes 786440 | tf_op jit(solution)/shard_map/ppermute | solution.py:281
  164.5 60.9 %copy-start.1 = (f32[4,128,512]{2,1,0:T(8,128)S(1)}, f32[4,128,512]{2,1,0:T(8,128)}, u32[]{:S(2)}) copy-start(f32[4,128,512]{2,1,0:T(8,128)} %parent.1) | copy-start | bytes 3145732
  172.7 12.6 %collective-permute-start.7 = (bf16[512,128]{1,0:T(8,128)(2,1)S(1)}, bf16[512,128]{1,0:T(8,128)(2,1)S(1)}, u32[]{:S(2)}, u32[]{:S(2)}) collective-permute-start(bf16[512,128]{1,0:T(8,128)(2,1)S(1)} %get-tuple-element.68), channel_id=1, source_target_pairs={{0,8},{1,9},{2,10},{3,11},{4,12},{5,13},{6,14},{7,15},{8,0},{9,1},... | collective-permute-start | bytes 393224 | tf_op jit(solution)/shard_map/ppermute | solution.py:281
  177.3 13.1 %collective-permute-start.8 = (bf16[512,128]{1,0:T(8,128)(2,1)S(1)}, bf16[512,128]{1,0:T(8,128)(2,1)S(1)}, u32[]{:S(2)}, u32[]{:S(2)}) collective-permute-start(bf16[512,128]{1,0:T(8,128)(2,1)S(1)} %get-tuple-element.69), channel_id=1, source_target_pairs={{0,12},{1,13},{2,14},{3,15},{4,0},{5,1},{6,2},{7,3},{8,4},{9,5},{1... | collective-permute-start | bytes 393224 | tf_op jit(solution)/shard_map/ppermute | solution.py:281
  177.3 14.7 %collective-permute-start.17 = (bf16[512,128]{1,0:T(8,128)(2,1)S(1)}, bf16[512,128]{1,0:T(8,128)(2,1)S(1)}, u32[]{:S(2)}, u32[]{:S(2)}) collective-permute-start(bf16[512,128]{1,0:T(8,128)(2,1)S(1)} %get-tuple-element.80), channel_id=1, source_target_pairs={{0,4},{1,5},{2,6},{3,7},{4,8},{5,9},{6,10},{7,11},{8,12},{9,13},{1... | collective-permute-start | bytes 393224 | tf_op jit(solution)/shard_map/ppermute | solution.py:281
  185.3 35.9 %collective-permute-start.18 = (bf16[512,128]{1,0:T(8,128)(2,1)S(1)}, bf16[512,128]{1,0:T(8,128)(2,1)S(1)}, u32[]{:S(2)}, u32[]{:S(2)}) collective-permute-start(bf16[512,128]{1,0:T(8,128)(2,1)S(1)} %get-tuple-element.81), channel_id=1, source_target_pairs={{0,8},{1,9},{2,10},{3,11},{4,12},{5,13},{6,14},{7,15},{8,0},{9,1},... | collective-permute-start | bytes 393224 | tf_op jit(solution)/shard_map/ppermute | solution.py:281
  190.3 30.9 %collective-permute-start.19 = (bf16[512,128]{1,0:T(8,128)(2,1)S(1)}, bf16[512,128]{1,0:T(8,128)(2,1)S(1)}, u32[]{:S(2)}, u32[]{:S(2)}) collective-permute-start(bf16[512,128]{1,0:T(8,128)(2,1)S(1)} %get-tuple-element.82), channel_id=1, source_target_pairs={{0,12},{1,13},{2,14},{3,15},{4,0},{5,1},{6,2},{7,3},{8,4},{9,5},{1... | collective-permute-start | bytes 393224 | tf_op jit(solution)/shard_map/ppermute | solution.py:281
  192.0 31.5 %collective-permute-start.28 = (bf16[512,128]{1,0:T(8,128)(2,1)S(1)}, bf16[512,128]{1,0:T(8,128)(2,1)S(1)}, u32[]{:S(2)}, u32[]{:S(2)}) collective-permute-start(bf16[512,128]{1,0:T(8,128)(2,1)S(1)} %get-tuple-element.93), channel_id=1, source_target_pairs={{0,4},{1,5},{2,6},{3,7},{4,8},{5,9},{6,10},{7,11},{8,12},{9,13},{1... | collective-permute-start | bytes 393224 | tf_op jit(solution)/shard_map/ppermute | solution.py:281
  211.7 13.7 %collective-permute-start.29 = (bf16[512,128]{1,0:T(8,128)(2,1)}, bf16[512,128]{1,0:T(8,128)(2,1)S(1)}, u32[]{:S(2)}, u32[]{:S(2)}) collective-permute-start(bf16[512,128]{1,0:T(8,128)(2,1)} %get-tuple-element.94), channel_id=1, source_target_pairs={{0,8},{1,9},{2,10},{3,11},{4,12},{5,13},{6,14},{7,15},{8,0},{9,1},... | collective-permute-start | bytes 393224 | tf_op jit(solution)/shard_map/ppermute | solution.py:281
  216.0 9.4 %collective-permute-start.30 = (bf16[512,128]{1,0:T(8,128)(2,1)}, bf16[512,128]{1,0:T(8,128)(2,1)S(1)}, u32[]{:S(2)}, u32[]{:S(2)}) collective-permute-start(bf16[512,128]{1,0:T(8,128)(2,1)} %get-tuple-element.95), channel_id=1, source_target_pairs={{0,12},{1,13},{2,14},{3,15},{4,0},{5,1},{6,2},{7,3},{8,4},{9,5},{1... | collective-permute-start | bytes 393224 | tf_op jit(solution)/shard_map/ppermute | solution.py:281
  221.2 7.3 %collective-permute-start.39 = (bf16[512,128]{1,0:T(8,128)(2,1)}, bf16[512,128]{1,0:T(8,128)(2,1)S(1)}, u32[]{:S(2)}, u32[]{:S(2)}) collective-permute-start(bf16[512,128]{1,0:T(8,128)(2,1)} %get-tuple-element.106), channel_id=1, source_target_pairs={{0,4},{1,5},{2,6},{3,7},{4,8},{5,9},{6,10},{7,11},{8,12},{9,13},{1... | collective-permute-start | bytes 393224 | tf_op jit(solution)/shard_map/ppermute | solution.py:281
  221.2 10.7 %collective-permute-start.40 = (bf16[512,128]{1,0:T(8,128)(2,1)}, bf16[512,128]{1,0:T(8,128)(2,1)S(1)}, u32[]{:S(2)}, u32[]{:S(2)}) collective-permute-start(bf16[512,128]{1,0:T(8,128)(2,1)} %get-tuple-element.107), channel_id=1, source_target_pairs={{0,8},{1,9},{2,10},{3,11},{4,12},{5,13},{6,14},{7,15},{8,0},{9,1},... | collective-permute-start | bytes 393224 | tf_op jit(solution)/shard_map/ppermute | solution.py:281
  223.6 10.1 %collective-permute-start.41 = (bf16[512,128]{1,0:T(8,128)(2,1)}, bf16[512,128]{1,0:T(8,128)(2,1)}, u32[]{:S(2)}, u32[]{:S(2)}) collective-permute-start(bf16[512,128]{1,0:T(8,128)(2,1)} %get-tuple-element.108), channel_id=1, source_target_pairs={{0,12},{1,13},{2,14},{3,15},{4,0},{5,1},{6,2},{7,3},{8,4},{9,5},{1... | collective-permute-start | bytes 393224 | tf_op jit(solution)/shard_map/ppermute | solution.py:281

commit v2 on v1

--- a/solution.py
+++ b/solution.py
@@ -288,8 +288,10 @@
     half = ROWS // 2
     lower = panels[:, :, :half]
     upper = lax.optimization_barrier(panels)[:, :, half:]
-    low_next, low_prev = over_y(lower, -1), over_y(lower, 1)
-    up_next, up_prev = over_y(upper, -1), over_y(upper, 1)
+    low_prev = over_y(lower, 1)
+    low_next = over_y(lower, -1)
+    up_prev = over_y(upper, 1)
+    up_next = over_y(upper, -1)
     low_far = over_y(low_next, -1)
     up_far = over_y(up_prev, 1)
     rights = [(), (low_next, low_prev), (up_next, up_prev), (low_far, up_far)]
@@ -302,7 +304,8 @@
         even, up, down = split(keep, swapped)
         parts = (even, over_z(up, 1, 0), over_z(down, -1, 0))
         merged = merge(parts)
-        summed.append([merged[0]] + [over_z(merged[h], 2 * h, 0) for h in range(1, HOPS)])
+        far = over_z(merged[2], 4, 0)
+        summed.append([merged[0], over_z(merged[1], 2, 0), far, over_z(merged[3], -2, 0)])
     sofar = finish(piece, parent, summed[:3])
     return finish_last(piece, sofar, summed[3])
 

time: 237 us -> 237 us (level)
  no operation moved by 1% of the time
where the time goes in v2:
time: 237 us
  waiting for transfers between devices  114 us (48%)
  starting transfers between devices  83.2 us (35%)
  Pallas kernels  34.4 us (15%)
  local copies, waits for them, and re-layouts  3.53 us (1%)
    ppermute x24, starting transfers between devices, over_z(): return lax.ppermute(v, ('z', 'core'), pairs)  63.2 us
    ppermute x12, waiting for transfers between devices, over_x(): return lax.ppermute(v, 'x', [(i, (i + dx) % NX) for i in range(NX)])  56.1 us
    ppermute x6, waiting for transfers between devices, over_y(): return lax.ppermute(v, 'grp', [(i, (i + d) % NY) for i in range(NY)])  35.9 us
    ppermute x24, waiting for transfers between devices, over_z(): return lax.ppermute(v, ('z', 'core'), pairs)  22.3 us
    pallas_call x4, Pallas kernels, products(): pl.pallas_call(functools.partial(products_kernel, parts=parts), in_specs=...  19.4 us
    ppermute x12, starting transfers between devices, over_x(): return lax.ppermute(v, 'x', [(i, (i + dx) % NX) for i in range(NX)])  12.5 us
    pallas_call x12, Pallas kernels, in_vmem(): pl.pallas_call(kernel, in_specs=[whole] * len(inputs), out_specs=[whole]...  10.5 us
    ppermute x6, starting transfers between devices, over_y(): return lax.ppermute(v, 'grp', [(i, (i + d) % NY) for i in range(NY)])  7.56 us
  transfers between devices with their start and end apart: 42, of which 14 were waited for; matrix products, arithmetic and copies ran while one was open for 0% of the time, Pallas kernels for 13%

profile of v2, /device:TPU:38, one launch (start us, length us, event | category | flops | bytes accessed | tf_op | source)
XLA Modules:
  0.0 236.5 jit_solution(3939377512747759797)
XLA Ops:
  0.0 2.4 %slice.6 = bf16[4,4,64,512]{3,2,1,0:T(8,128)(2,1)} slice(bf16[4,4,128,512]{3,2,1,0:T(8,128)(2,1)} %left.7), slice={[0:4], [0:4], [0:64], [0:512]} | slice | bytes 2097152 | tf_op jit(solution)/shard_map/slice | solution.py:289
  2.5 3.0 %collective-permute-start.9 = (bf16[4,4,64,512]{3,2,1,0:T(8,128)(2,1)}, bf16[4,4,64,512]{3,2,1,0:T(8,128)(2,1)S(1)}, u32[]{:S(2)}, u32[]{:S(2)}) collective-permute-start(bf16[4,4,64,512]{3,2,1,0:T(8,128)(2,1)} %slice.6), channel_id=1, source_target_pairs={{0,192},{64,0},{128,64},{192,128},{1,193},{65,1},{129,65},{193,129... | collective-permute-start | bytes 3145736 | tf_op jit(solution)/shard_map/ppermute | solution.py:272
  5.5 1.1 slice.8
  7.1 2.7 %collective-permute-start.20 = (bf16[4,4,64,512]{3,2,1,0:T(8,128)(2,1)}, bf16[4,4,64,512]{3,2,1,0:T(8,128)(2,1)}, u32[]{:S(2)}, u32[]{:S(2)}) collective-permute-start(bf16[4,4,64,512]{3,2,1,0:T(8,128)(2,1)} %slice.8), channel_id=1, source_target_pairs={{0,192},{64,0},{128,64},{192,128},{1,193},{65,1},{129,65},{193,129... | collective-permute-start | bytes 3145736 | tf_op jit(solution)/shard_map/ppermute | solution.py:272
  10.5 4.4 %products.4 = (bf16[2064,128]{1,0:T(8,128)(2,1)S(1)}, bf16[2064,128]{1,0:T(8,128)(2,1)S(1)}, bf16[2064,128]{1,0:T(8,128)(2,1)S(1)}, bf16[2064,128]{1,0:T(8,128)(2,1)S(1)}) custom-call(s32[3]{0:T(128)S(1)} %pad_add_fusion.place, s32[40]{0:T(128)S(1)} %bitcast.6, s32[40]{0:T(128)S(1)} %bitcast.10, s32[40]{0:T(128)S(1)} %copy-done.4, s32[1]{0:T(128)S(6)} %copy.9.count, ...), custom_call_target="tpu_custom_call" | custom-call | flops 671088640 | bytes 6291456 | tf_op jit(solution)/shard_map/products/pallas_call | solution.py:87
  15.5 13.8 %collective-permute-done.9.rest_0_ = bf16[4,4,64,512]{3,2,1,0:T(8,128)(2,1)S(1)} collective-permute-done((bf16[4,4,64,512]{3,2,1,0:T(8,128)(2,1)}, bf16[4,4,64,512]{3,2,1,0:T(8,128)(2,1)S(1)}, u32[]{:S(2)}, u32[]{:S(2)}) %collective-permute-start.9) | collective-permute-done | bytes 1048608 | tf_op jit(solution)/shard_map/ppermute | solution.py:272
  29.3 1.4 collective-permute-start.1
  30.7 2.3 collective-permute-done.10.rest_1_
  33.0 1.3 collective-permute-start.31
  34.3 19.8 %collective-permute-done.21.rest_1_ = bf16[4,4,64,512]{3,2,1,0:T(8,128)(2,1)} collective-permute-done((bf16[4,4,64,512]{3,2,1,0:T(8,128)(2,1)}, bf16[4,4,64,512]{3,2,1,0:T(8,128)(2,1)}, u32[]{:S(2)}, u32[]{:S(2)}) %collective-permute-start.21) | collective-permute-done | bytes 1048608 | tf_op jit(solution)/shard_map/ppermute | solution.py:272
  54.1 5.1 %products.5 = (bf16[2064,128]{1,0:T(8,128)(2,1)S(1)}, bf16[2064,128]{1,0:T(8,128)(2,1)S(1)}, bf16[2064,128]{1,0:T(8,128)(2,1)S(1)}, bf16[2064,128]{1,0:T(8,128)(2,1)S(1)}) custom-call(s32[3]{0:T(128)S(1)} %pad_add_fusion.place, s32[40]{0:T(128)S(1)} %bitcast.7, s32[40]{0:T(128)S(1)} %bitcast.11, s32[40]{0:T(128)S(1)} %copy-done.4, s32[1]{0:T(128)S(6)} %copy.9.count, ...), custom_call_target="tpu_custom_call" | custom-call | flops 671088640 | bytes 6291456 | tf_op jit(solution)/shard_map/products/pallas_call | solution.py:87
  60.1 2.4 %collective-permute-start.11 = (bf16[2064,128]{1,0:T(8,128)(2,1)S(1)}, bf16[2064,128]{1,0:T(8,128)(2,1)S(1)}, u32[]{:S(2)}, u32[]{:S(2)}) collective-permute-start(bf16[2064,128]{1,0:T(8,128)(2,1)S(1)} %get-tuple-element.71), channel_id=1, source_target_pairs={{0,16},{16,32},{32,48},{48,0},{1,17},{17,33},{33,49},{49,1},{2,18}... | collective-permute-start | bytes 1585160 | tf_op jit(solution)/shard_map/ppermute | solution.py:276
  62.7 5.4 %products.6 = (bf16[2064,128]{1,0:T(8,128)(2,1)S(1)}, bf16[2064,128]{1,0:T(8,128)(2,1)S(1)}, bf16[2064,128]{1,0:T(8,128)(2,1)S(1)}, bf16[2064,128]{1,0:T(8,128)(2,1)S(1)}) custom-call(s32[3]{0:T(128)S(1)} %pad_add_fusion.place, s32[40]{0:T(128)S(1)} %bitcast.8, s32[40]{0:T(128)S(1)} %bitcast.12, s32[40]{0:T(128)S(1)} %copy-done.4, s32[1]{0:T(128)S(6)} %copy.9.count, ...), custom_call_target="tpu_custom_call" | custom-call | flops 671088640 | bytes 6291456 | tf_op jit(solution)/shard_map/products/pallas_call | solution.py:87
  68.2 17.5 %collective-permute-done.2.refs_3_ = bf16[2064,128]{1,0:T(8,128)(2,1)S(1)} collective-permute-done((bf16[2064,128]{1,0:T(8,128)(2,1)S(1)}, bf16[2064,128]{1,0:T(8,128)(2,1)S(1)}, u32[]{:S(2)}, u32[]{:S(2)}) %collective-permute-start.2) | collective-permute-done | bytes 528416 | tf_op jit(solution)/shard_map/ppermute | solution.py:276
  85.7 3.2 %collective-permute-start.22 = (bf16[2064,128]{1,0:T(8,128)(2,1)S(1)}, bf16[2064,128]{1,0:T(8,128)(2,1)S(1)}, u32[]{:S(2)}, u32[]{:S(2)}) collective-permute-start(bf16[2064,128]{1,0:T(8,128)(2,1)S(1)} %get-tuple-element.84), channel_id=1, source_target_pairs={{0,16},{16,32},{32,48},{48,0},{1,17},{17,33},{33,49},{49,1},{2,18}... | collective-permute-start | bytes 1585160 | tf_op jit(solution)/shard_map/ppermute | solution.py:276
  89.8 4.4 %products.7 = (bf16[2064,128]{1,0:T(8,128)(2,1)S(1)}, bf16[2064,128]{1,0:T(8,128)(2,1)S(1)}, bf16[2064,128]{1,0:T(8,128)(2,1)S(1)}, bf16[2064,128]{1,0:T(8,128)(2,1)S(1)}) custom-call(s32[3]{0:T(128)S(1)} %pad_add_fusion.place, s32[40]{0:T(128)S(1)} %bitcast.9, s32[40]{0:T(128)S(1)} %bitcast.13, s32[40]{0:T(128)S(1)} %copy-done.4, s32[1]{0:T(128)S(6)} %copy.9.count, ...), custom_call_target="tpu_custom_call" | custom-call | flops 671088640 | bytes 6291456 | tf_op jit(solution)/shard_map/products/pallas_call | solution.py:87
  94.3 2.6 %collective-permute-start.33 = (bf16[2064,128]{1,0:T(8,128)(2,1)S(1)}, bf16[2064,128]{1,0:T(8,128)(2,1)S(1)}, u32[]{:S(2)}, u32[]{:S(2)}) collective-permute-start(bf16[2064,128]{1,0:T(8,128)(2,1)S(1)} %get-tuple-element.97), channel_id=1, source_target_pairs={{0,16},{16,32},{32,48},{48,0},{1,17},{17,33},{33,49},{49,1},{2,18}... | collective-permute-start | bytes 1585160 | tf_op jit(solution)/shard_map/ppermute | solution.py:276
  96.9 16.1 %collective-permute-done.13.refs_3_ = bf16[2064,128]{1,0:T(8,128)(2,1)S(1)} collective-permute-done((bf16[2064,128]{1,0:T(8,128)(2,1)S(1)}, bf16[2064,128]{1,0:T(8,128)(2,1)S(1)}, u32[]{:S(2)}, u32[]{:S(2)}) %collective-permute-start.13) | collective-permute-done | bytes 528416 | tf_op jit(solution)/shard_map/ppermute | solution.py:276
  113.2 1.5 shard_map.64
  114.9 1.5 shard_map.67
  116.4 19.0 %collective-permute-done.24.refs_3_ = bf16[2064,128]{1,0:T(8,128)(2,1)S(1)} collective-permute-done((bf16[2064,128]{1,0:T(8,128)(2,1)S(1)}, bf16[2064,128]{1,0:T(8,128)(2,1)S(1)}, u32[]{:S(2)}, u32[]{:S(2)}) %collective-permute-start.24) | collective-permute-done | bytes 528416 | tf_op jit(solution)/shard_map/ppermute | solution.py:276
  135.4 1.5 shard_map.70
  137.6 3.5 %collective-permute-done.35.refs_3_ = bf16[2064,128]{1,0:T(8,128)(2,1)S(1)} collective-permute-done((bf16[2064,128]{1,0:T(8,128)(2,1)S(1)}, bf16[2064,128]{1,0:T(8,128)(2,1)S(1)}, u32[]{:S(2)}, u32[]{:S(2)}) %collective-permute-start.35) | collective-permute-done | bytes 528416 | tf_op jit(solution)/shard_map/ppermute | solution.py:276
  141.1 1.5 shard_map.73
  143.2 2.0 collective-permute-start.4
  145.8 2.0 collective-permute-start.15
  147.8 2.2 collective-permute-start.16
  150.5 1.9 collective-permute-done.4.up
  152.5 1.9 collective-permute-start.26
  154.4 2.0 collective-permute-start.27
  156.7 3.8 %collective-permute-start.6 = (bf16[512,128]{1,0:T(8,128)(2,1)S(1)}, bf16[512,128]{1,0:T(8,128)(2,1)S(1)}, u32[]{:S(2)}, u32[]{:S(2)}) collective-permute-start(bf16[512,128]{1,0:T(8,128)(2,1)S(1)} %get-tuple-element.67), channel_id=1, source_target_pairs={{0,4},{1,5},{2,6},{3,7},{4,8},{5,9},{6,10},{7,11},{8,12},{9,13},{1... | collective-permute-start | bytes 393224 | tf_op jit(solution)/shard_map/ppermute | solution.py:281
  160.9 3.5 %collective-permute-start.37 = (bf16[1024,128]{1,0:T(8,128)(2,1)S(1)}, bf16[1024,128]{1,0:T(8,128)(2,1)S(1)}, u32[]{:S(2)}, u32[]{:S(2)}) collective-permute-start(bf16[1024,128]{1,0:T(8,128)(2,1)S(1)} %get-tuple-element.103), channel_id=1, source_target_pairs={{0,2},{1,3},{2,4},{3,5},{4,6},{5,7},{6,8},{7,9},{8,10},{9,11},{10,... | collective-permute-start | bytes 786440 | tf_op jit(solution)/shard_map/ppermute | solution.py:281
  164.7 8.0 %collective-permute-done.6.refs_1_ = bf16[512,128]{1,0:T(8,128)(2,1)S(1)} collective-permute-done((bf16[512,128]{1,0:T(8,128)(2,1)S(1)}, bf16[512,128]{1,0:T(8,128)(2,1)S(1)}, u32[]{:S(2)}, u32[]{:S(2)}) %collective-permute-start.6) | collective-permute-done | bytes 131104 | tf_op jit(solution)/shard_map/ppermute | solution.py:281
  172.7 4.6 %collective-permute-start.7 = (bf16[512,128]{1,0:T(8,128)(2,1)S(1)}, bf16[512,128]{1,0:T(8,128)(2,1)S(1)}, u32[]{:S(2)}, u32[]{:S(2)}) collective-permute-start(bf16[512,128]{1,0:T(8,128)(2,1)S(1)} %get-tuple-element.68), channel_id=1, source_target_pairs={{0,8},{1,9},{2,10},{3,11},{4,12},{5,13},{6,14},{7,15},{8,0},{9,1},... | collective-permute-start | bytes 393224 | tf_op jit(solution)/shard_map/ppermute | solution.py:281
  177.3 2.9 %collective-permute-start.17 = (bf16[512,128]{1,0:T(8,128)(2,1)S(1)}, bf16[512,128]{1,0:T(8,128)(2,1)S(1)}, u32[]{:S(2)}, u32[]{:S(2)}) collective-permute-start(bf16[512,128]{1,0:T(8,128)(2,1)S(1)} %get-tuple-element.80), channel_id=1, source_target_pairs={{0,4},{1,5},{2,6},{3,7},{4,8},{5,9},{6,10},{7,11},{8,12},{9,13},{1... | collective-permute-start | bytes 393224 | tf_op jit(solution)/shard_map/ppermute | solution.py:281
  181.2 4.2 %collective-permute-done.7.refs_2_ = bf16[512,128]{1,0:T(8,128)(2,1)S(1)} collective-permute-done((bf16[512,128]{1,0:T(8,128)(2,1)S(1)}, bf16[512,128]{1,0:T(8,128)(2,1)S(1)}, u32[]{:S(2)}, u32[]{:S(2)}) %collective-permute-start.7) | collective-permute-done | bytes 131104 | tf_op jit(solution)/shard_map/ppermute | solution.py:281
  185.3 5.0 %collective-permute-start.18 = (bf16[512,128]{1,0:T(8,128)(2,1)S(1)}, bf16[512,128]{1,0:T(8,128)(2,1)S(1)}, u32[]{:S(2)}, u32[]{:S(2)}) collective-permute-start(bf16[512,128]{1,0:T(8,128)(2,1)S(1)} %get-tuple-element.81), channel_id=1, source_target_pairs={{0,8},{1,9},{2,10},{3,11},{4,12},{5,13},{6,14},{7,15},{8,0},{9,1},... | collective-permute-start | bytes 393224 | tf_op jit(solution)/shard_map/ppermute | solution.py:281
  190.3 1.7 collective-permute-done.17.refs_5_
  192.0 19.7 %collective-permute-start.28 = (bf16[512,128]{1,0:T(8,128)(2,1)S(1)}, bf16[512,128]{1,0:T(8,128)(2,1)S(1)}, u32[]{:S(2)}, u32[]{:S(2)}) collective-permute-start(bf16[512,128]{1,0:T(8,128)(2,1)S(1)} %get-tuple-element.93), channel_id=1, source_target_pairs={{0,4},{1,5},{2,6},{3,7},{4,8},{5,9},{6,10},{7,11},{8,12},{9,13},{1... | collective-permute-start | bytes 393224 | tf_op jit(solution)/shard_map/ppermute | solution.py:281
  211.7 4.3 %collective-permute-start.29 = (bf16[512,128]{1,0:T(8,128)(2,1)}, bf16[512,128]{1,0:T(8,128)(2,1)S(1)}, u32[]{:S(2)}, u32[]{:S(2)}) collective-permute-start(bf16[512,128]{1,0:T(8,128)(2,1)} %get-tuple-element.94), channel_id=1, source_target_pairs={{0,8},{1,9},{2,10},{3,11},{4,12},{5,13},{6,14},{7,15},{8,0},{9,1},... | collective-permute-start | bytes 393224 | tf_op jit(solution)/shard_map/ppermute | solution.py:281
  216.0 4.1 %collective-permute-start.30 = (bf16[512,128]{1,0:T(8,128)(2,1)}, bf16[512,128]{1,0:T(8,128)(2,1)S(1)}, u32[]{:S(2)}, u32[]{:S(2)}) collective-permute-start(bf16[512,128]{1,0:T(8,128)(2,1)} %get-tuple-element.95), channel_id=1, source_target_pairs={{0,12},{1,13},{2,14},{3,15},{4,0},{5,1},{6,2},{7,3},{8,4},{9,5},{1... | collective-permute-start | bytes 393224 | tf_op jit(solution)/shard_map/ppermute | solution.py:281
  221.2 2.4 collective-permute-start.40
  223.6 1.9 collective-permute-start.41
  225.4 1.8 finish.1.sofar
  227.3 1.2 collective-permute-done.39.refs_1_
  228.5 3.4 %collective-permute-done.40.refs_2_ = bf16[512,128]{1,0:T(8,128)(2,1)S(1)} collective-permute-done((bf16[512,128]{1,0:T(8,128)(2,1)}, bf16[512,128]{1,0:T(8,128)(2,1)S(1)}, u32[]{:S(2)}, u32[]{:S(2)}) %collective-permute-start.40) | collective-permute-done | bytes 131104 | tf_op jit(solution)/shard_map/ppermute | solution.py:281
  231.9 1.8 collective-permute-done.41.refs_3_
  233.7 2.6 %finish_last.1 = f32[4,128,512]{2,1,0:T(8,128)} custom-call(s32[1]{0:T(128)} %bitcast.piece, f32[4,128,512]{2,1,0:T(8,128)} %finish.1.sofar, f32[512,128]{1,0:T(8,128)S(1)} %get-tuple-element.105.refs_0_, bf16[512,128]{1,0:T(8,128)(2,1)S(1)} %collective-permute-done.39.refs_1_, ...), custom_call_target="tpu_custom_call", output_to_operand_aliasing={{}: (1, {})} | custom-call | flops 655360 | bytes 2097152 | tf_op jit(solution)/shard_map/finish_last/pallas_call | solution.py:254
  (67 shorter events, 8.9 us)
Async XLA Ops:
  0.0 5.5 %copy-start = (bf16[4,4,128,512]{3,2,1,0:T(8,128)(2,1)S(1)}, bf16[4,4,128,512]{3,2,1,0:T(8,128)(2,1)}, u32[]{:S(2)}) copy-start(bf16[4,4,128,512]{3,2,1,0:T(8,128)(2,1)} %left.7) | copy-start | bytes 6291460
  0.0 10.5 %copy-start.2 = (s32[1,40]{1,0:T(1,128)S(1)}, s32[1,40]{1,0:T(1,128)}, u32[]{:S(2)}) copy-start(s32[1,40]{1,0:T(1,128)} %param.8) | copy-start | bytes 484
  0.0 10.5 %copy-start.3 = (s32[40,1]{0,1:T(1,128)S(1)}, s32[40,1]{0,1:T(1,128)}, u32[]{:S(2)}) copy-start(s32[40,1]{0,1:T(1,128)} %param.9) | copy-start | bytes 484
  0.0 10.5 %copy-start.4 = (s32[40]{0:T(128)S(1)}, s32[40]{0:T(128)}, u32[]{:S(2)}) copy-start(s32[40]{0:T(128)} %target.7) | copy-start | bytes 484
  2.5 26.9 %collective-permute-start.9 = (bf16[4,4,64,512]{3,2,1,0:T(8,128)(2,1)}, bf16[4,4,64,512]{3,2,1,0:T(8,128)(2,1)S(1)}, u32[]{:S(2)}, u32[]{:S(2)}) collective-permute-start(bf16[4,4,64,512]{3,2,1,0:T(8,128)(2,1)} %slice.6), channel_id=1, source_target_pairs={{0,192},{64,0},{128,64},{192,128},{1,193},{65,1},{129,65},{193,129... | collective-permute-start | bytes 3145736 | tf_op jit(solution)/shard_map/ppermute | solution.py:272
  5.5 27.6 %collective-permute-start.10 = (bf16[4,4,64,512]{3,2,1,0:T(8,128)(2,1)}, bf16[4,4,64,512]{3,2,1,0:T(8,128)(2,1)}, u32[]{:S(2)}, u32[]{:S(2)}) collective-permute-start(bf16[4,4,64,512]{3,2,1,0:T(8,128)(2,1)} %slice.6), channel_id=1, source_target_pairs={{0,64},{64,128},{128,192},{192,0},{1,65},{65,129},{129,193},{193,1... | collective-permute-start | bytes 3145736 | tf_op jit(solution)/shard_map/ppermute | solution.py:272
  6.6 47.5 %collective-permute-start.21 = (bf16[4,4,64,512]{3,2,1,0:T(8,128)(2,1)}, bf16[4,4,64,512]{3,2,1,0:T(8,128)(2,1)}, u32[]{:S(2)}, u32[]{:S(2)}) collective-permute-start(bf16[4,4,64,512]{3,2,1,0:T(8,128)(2,1)} %slice.8), channel_id=1, source_target_pairs={{0,64},{64,128},{128,192},{192,0},{1,65},{65,129},{129,193},{193,1... | collective-permute-start | bytes 3145736 | tf_op jit(solution)/shard_map/ppermute | solution.py:272
  7.1 55.4 %collective-permute-start.20 = (bf16[4,4,64,512]{3,2,1,0:T(8,128)(2,1)}, bf16[4,4,64,512]{3,2,1,0:T(8,128)(2,1)}, u32[]{:S(2)}, u32[]{:S(2)}) collective-permute-start(bf16[4,4,64,512]{3,2,1,0:T(8,128)(2,1)} %slice.8), channel_id=1, source_target_pairs={{0,192},{64,0},{128,64},{192,128},{1,193},{65,1},{129,65},{193,129... | collective-permute-start | bytes 3145736 | tf_op jit(solution)/shard_map/ppermute | solution.py:272
  15.0 44.2 %collective-permute-start = (bf16[2064,128]{1,0:T(8,128)(2,1)S(1)}, bf16[2064,128]{1,0:T(8,128)(2,1)S(1)}, u32[]{:S(2)}, u32[]{:S(2)}) collective-permute-start(bf16[2064,128]{1,0:T(8,128)(2,1)S(1)} %get-tuple-element.58), channel_id=1, source_target_pairs={{0,16},{16,32},{32,48},{48,0},{1,17},{17,33},{33,49},{49,1},{2,18}... | collective-permute-start | bytes 1585160 | tf_op jit(solution)/shard_map/ppermute | solution.py:276
  29.3 30.8 %collective-permute-start.1 = (bf16[2064,128]{1,0:T(8,128)(2,1)S(1)}, bf16[2064,128]{1,0:T(8,128)(2,1)S(1)}, u32[]{:S(2)}, u32[]{:S(2)}) collective-permute-start(bf16[2064,128]{1,0:T(8,128)(2,1)S(1)} %get-tuple-element.59), channel_id=1, source_target_pairs={{0,32},{16,48},{32,0},{48,16},{1,33},{17,49},{33,1},{49,17},{2,34}... | collective-permute-start | bytes 1585160 | tf_op jit(solution)/shard_map/ppermute | solution.py:276
  33.0 55.9 %collective-permute-start.31 = (bf16[4,4,64,512]{3,2,1,0:T(8,128)(2,1)S(1)}, bf16[4,4,64,512]{3,2,1,0:T(8,128)(2,1)S(1)}, u32[]{:S(2)}, u32[]{:S(2)}) collective-permute-start(bf16[4,4,64,512]{3,2,1,0:T(8,128)(2,1)S(1)} %collective-permute-done.9.rest_0_), channel_id=1, source_target_pairs={{0,192},{64,0},{128,64},{192,128},{1,193},{65,1},{129,65},{193,129... | collective-permute-start | bytes 3145736 | tf_op jit(solution)/shard_map/ppermute | solution.py:272
  54.1 34.8 %collective-permute-start.32 = (bf16[4,4,64,512]{3,2,1,0:T(8,128)(2,1)}, bf16[4,4,64,512]{3,2,1,0:T(8,128)(2,1)S(1)}, u32[]{:S(2)}, u32[]{:S(2)}) collective-permute-start(bf16[4,4,64,512]{3,2,1,0:T(8,128)(2,1)} %collective-permute-done.21.rest_1_), channel_id=1, source_target_pairs={{0,64},{64,128},{128,192},{192,0},{1,65},{65,129},{129,193},{193,1... | collective-permute-start | bytes 3145736 | tf_op jit(solution)/shard_map/ppermute | solution.py:272
  59.2 26.4 %collective-permute-start.2 = (bf16[2064,128]{1,0:T(8,128)(2,1)S(1)}, bf16[2064,128]{1,0:T(8,128)(2,1)S(1)}, u32[]{:S(2)}, u32[]{:S(2)}) collective-permute-start(bf16[2064,128]{1,0:T(8,128)(2,1)S(1)} %get-tuple-element.60), channel_id=1, source_target_pairs={{0,48},{16,0},{32,16},{48,32},{1,49},{17,1},{33,17},{49,33},{2,50}... | collective-permute-start | bytes 1585160 | tf_op jit(solution)/shard_map/ppermute | solution.py:276
  60.1 25.5 %collective-permute-start.11 = (bf16[2064,128]{1,0:T(8,128)(2,1)S(1)}, bf16[2064,128]{1,0:T(8,128)(2,1)S(1)}, u32[]{:S(2)}, u32[]{:S(2)}) collective-permute-start(bf16[2064,128]{1,0:T(8,128)(2,1)S(1)} %get-tuple-element.71), channel_id=1, source_target_pairs={{0,16},{16,32},{32,48},{48,0},{1,17},{17,33},{33,49},{49,1},{2,18}... | collective-permute-start | bytes 1585160 | tf_op jit(solution)/shard_map/ppermute | solution.py:276
  62.5 31.8 %collective-permute-start.12 = (bf16[2064,128]{1,0:T(8,128)(2,1)S(1)}, bf16[2064,128]{1,0:T(8,128)(2,1)S(1)}, u32[]{:S(2)}, u32[]{:S(2)}) collective-permute-start(bf16[2064,128]{1,0:T(8,128)(2,1)S(1)} %get-tuple-element.72), channel_id=1, source_target_pairs={{0,32},{16,48},{32,0},{48,16},{1,33},{17,49},{33,1},{49,17},{2,34}... | collective-permute-start | bytes 1585160 | tf_op jit(solution)/shard_map/ppermute | solution.py:276
  85.6 27.4 %collective-permute-start.13 = (bf16[2064,128]{1,0:T(8,128)(2,1)S(1)}, bf16[2064,128]{1,0:T(8,128)(2,1)S(1)}, u32[]{:S(2)}, u32[]{:S(2)}) collective-permute-start(bf16[2064,128]{1,0:T(8,128)(2,1)S(1)} %get-tuple-element.73), channel_id=1, source_target_pairs={{0,48},{16,0},{32,16},{48,32},{1,49},{17,1},{33,17},{49,33},{2,50}... | collective-permute-start | bytes 1585160 | tf_op jit(solution)/shard_map/ppermute | solution.py:276
  85.7 27.4 %collective-permute-start.22 = (bf16[2064,128]{1,0:T(8,128)(2,1)S(1)}, bf16[2064,128]{1,0:T(8,128)(2,1)S(1)}, u32[]{:S(2)}, u32[]{:S(2)}) collective-permute-start(bf16[2064,128]{1,0:T(8,128)(2,1)S(1)} %get-tuple-element.84), channel_id=1, source_target_pairs={{0,16},{16,32},{32,48},{48,0},{1,17},{17,33},{33,49},{49,1},{2,18}... | collective-permute-start | bytes 1585160 | tf_op jit(solution)/shard_map/ppermute | solution.py:276
  88.9 25.9 %collective-permute-start.23 = (bf16[2064,128]{1,0:T(8,128)(2,1)S(1)}, bf16[2064,128]{1,0:T(8,128)(2,1)S(1)}, u32[]{:S(2)}, u32[]{:S(2)}) collective-permute-start(bf16[2064,128]{1,0:T(8,128)(2,1)S(1)} %get-tuple-element.85), channel_id=1, source_target_pairs={{0,32},{16,48},{32,0},{48,16},{1,33},{17,49},{33,1},{49,17},{2,34}... | collective-permute-start | bytes 1585160 | tf_op jit(solution)/shard_map/ppermute | solution.py:276
  88.9 46.5 %collective-permute-start.24 = (bf16[2064,128]{1,0:T(8,128)(2,1)S(1)}, bf16[2064,128]{1,0:T(8,128)(2,1)S(1)}, u32[]{:S(2)}, u32[]{:S(2)}) collective-permute-start(bf16[2064,128]{1,0:T(8,128)(2,1)S(1)} %get-tuple-element.86), channel_id=1, source_target_pairs={{0,48},{16,0},{32,16},{48,32},{1,49},{17,1},{33,17},{49,33},{2,50}... | collective-permute-start | bytes 1585160 | tf_op jit(solution)/shard_map/ppermute | solution.py:276
  94.3 42.6 %collective-permute-start.33 = (bf16[2064,128]{1,0:T(8,128)(2,1)S(1)}, bf16[2064,128]{1,0:T(8,128)(2,1)S(1)}, u32[]{:S(2)}, u32[]{:S(2)}) collective-permute-start(bf16[2064,128]{1,0:T(8,128)(2,1)S(1)} %get-tuple-element.97), channel_id=1, source_target_pairs={{0,16},{16,32},{32,48},{48,0},{1,17},{17,33},{33,49},{49,1},{2,18}... | collective-permute-start | bytes 1585160 | tf_op jit(solution)/shard_map/ppermute | solution.py:276
  113.0 24.5 %collective-permute-start.34 = (bf16[2064,128]{1,0:T(8,128)(2,1)S(1)}, bf16[2064,128]{1,0:T(8,128)(2,1)S(1)}, u32[]{:S(2)}, u32[]{:S(2)}) collective-permute-start(bf16[2064,128]{1,0:T(8,128)(2,1)S(1)} %get-tuple-element.98), channel_id=1, source_target_pairs={{0,32},{16,48},{32,0},{48,16},{1,33},{17,49},{33,1},{49,17},{2,34}... | collective-permute-start | bytes 1585160 | tf_op jit(solution)/shard_map/ppermute | solution.py:276
  113.0 28.0 %collective-permute-start.35 = (bf16[2064,128]{1,0:T(8,128)(2,1)S(1)}, bf16[2064,128]{1,0:T(8,128)(2,1)S(1)}, u32[]{:S(2)}, u32[]{:S(2)}) collective-permute-start(bf16[2064,128]{1,0:T(8,128)(2,1)S(1)} %get-tuple-element.99), channel_id=1, source_target_pairs={{0,48},{16,0},{32,16},{48,32},{1,49},{17,1},{33,17},{49,33},{2,50}... | collective-permute-start | bytes 1585160 | tf_op jit(solution)/shard_map/ppermute | solution.py:276
  114.8 27.9 %collective-permute-start.3 = (bf16[4096,128]{1,0:T(8,128)(2,1)S(1)}, bf16[4096,128]{1,0:T(8,128)(2,1)S(1)}, u32[]{:S(2)}, u32[]{:S(2)}) collective-permute-start(bf16[4096,128]{1,0:T(8,128)(2,1)S(1)} %get-tuple-element.62), channel_id=1, source_target_pairs={{0,1},{1,0},{2,3},{3,2},{4,5},{5,4},{6,7},{7,6},{8,9},{9,8},{10,11... | collective-permute-start | bytes 3145736 | tf_op jit(solution)/shard_map/ppermute | solution.py:281
  135.4 9.9 %collective-permute-start.14 = (bf16[4096,128]{1,0:T(8,128)(2,1)S(1)}, bf16[4096,128]{1,0:T(8,128)(2,1)S(1)}, u32[]{:S(2)}, u32[]{:S(2)}) collective-permute-start(bf16[4096,128]{1,0:T(8,128)(2,1)S(1)} %get-tuple-element.75), channel_id=1, source_target_pairs={{0,1},{1,0},{2,3},{3,2},{4,5},{5,4},{6,7},{7,6},{8,9},{9,8},{10,11... | collective-permute-start | bytes 3145736 | tf_op jit(solution)/shard_map/ppermute | solution.py:281
  137.0 10.9 %collective-permute-start.25 = (bf16[4096,128]{1,0:T(8,128)(2,1)S(1)}, bf16[4096,128]{1,0:T(8,128)(2,1)S(1)}, u32[]{:S(2)}, u32[]{:S(2)}) collective-permute-start(bf16[4096,128]{1,0:T(8,128)(2,1)S(1)} %get-tuple-element.88), channel_id=1, source_target_pairs={{0,1},{1,0},{2,3},{3,2},{4,5},{5,4},{6,7},{7,6},{8,9},{9,8},{10,11... | collective-permute-start | bytes 3145736 | tf_op jit(solution)/shard_map/ppermute | solution.py:281
  142.6 14.1 %collective-permute-start.36 = (bf16[4096,128]{1,0:T(8,128)(2,1)S(1)}, bf16[4096,128]{1,0:T(8,128)(2,1)S(1)}, u32[]{:S(2)}, u32[]{:S(2)}) collective-permute-start(bf16[4096,128]{1,0:T(8,128)(2,1)S(1)} %get-tuple-element.101), channel_id=1, source_target_pairs={{0,1},{1,0},{2,3},{3,2},{4,5},{5,4},{6,7},{7,6},{8,9},{9,8},{10,11... | collective-permute-start | bytes 3145736 | tf_op jit(solution)/shard_map/ppermute | solution.py:281
  143.2 9.3 %collective-permute-start.4 = (bf16[1024,128]{1,0:T(8,128)(2,1)S(1)}, bf16[1024,128]{1,0:T(8,128)(2,1)S(1)}, u32[]{:S(2)}, u32[]{:S(2)}) collective-permute-start(bf16[1024,128]{1,0:T(8,128)(2,1)S(1)} %get-tuple-element.64), channel_id=1, source_target_pairs={{0,2},{1,3},{2,4},{3,5},{4,6},{5,7},{6,8},{7,9},{8,10},{9,11},{10,... | collective-permute-start | bytes 786440 | tf_op jit(solution)/shard_map/ppermute | solution.py:281
  145.2 9.2 %collective-permute-start.5 = (bf16[1024,128]{1,0:T(8,128)(2,1)S(1)}, bf16[1024,128]{1,0:T(8,128)(2,1)S(1)}, u32[]{:S(2)}, u32[]{:S(2)}) collective-permute-start(bf16[1024,128]{1,0:T(8,128)(2,1)S(1)} %get-tuple-element.65), channel_id=1, source_target_pairs={{0,14},{1,15},{2,0},{3,1},{4,2},{5,3},{6,4},{7,5},{8,6},{9,7},{10,... | collective-permute-start | bytes 786440 | tf_op jit(solution)/shard_map/ppermute | solution.py:281
  145.8 15.1 %collective-permute-start.15 = (bf16[1024,128]{1,0:T(8,128)(2,1)S(1)}, bf16[1024,128]{1,0:T(8,128)(2,1)S(1)}, u32[]{:S(2)}, u32[]{:S(2)}) collective-permute-start(bf16[1024,128]{1,0:T(8,128)(2,1)S(1)} %get-tuple-element.77), channel_id=1, source_target_pairs={{0,2},{1,3},{2,4},{3,5},{4,6},{5,7},{6,8},{7,9},{8,10},{9,11},{10,... | collective-permute-start | bytes 786440 | tf_op jit(solution)/shard_map/ppermute | solution.py:281
  147.8 16.7 %collective-permute-start.16 = (bf16[1024,128]{1,0:T(8,128)(2,1)S(1)}, bf16[1024,128]{1,0:T(8,128)(2,1)S(1)}, u32[]{:S(2)}, u32[]{:S(2)}) collective-permute-start(bf16[1024,128]{1,0:T(8,128)(2,1)S(1)} %get-tuple-element.78), channel_id=1, source_target_pairs={{0,14},{1,15},{2,0},{3,1},{4,2},{5,3},{6,4},{7,5},{8,6},{9,7},{10,... | collective-permute-start | bytes 786440 | tf_op jit(solution)/shard_map/ppermute | solution.py:281
  152.5 24.8 %collective-permute-start.26 = (bf16[1024,128]{1,0:T(8,128)(2,1)S(1)}, bf16[1024,128]{1,0:T(8,128)(2,1)S(1)}, u32[]{:S(2)}, u32[]{:S(2)}) collective-permute-start(bf16[1024,128]{1,0:T(8,128)(2,1)S(1)} %get-tuple-element.90), channel_id=1, source_target_pairs={{0,2},{1,3},{2,4},{3,5},{4,6},{5,7},{6,8},{7,9},{8,10},{9,11},{10,... | collective-permute-start | bytes 786440 | tf_op jit(solution)/shard_map/ppermute | solution.py:281
  154.4 22.9 %collective-permute-start.27 = (bf16[1024,128]{1,0:T(8,128)(2,1)S(1)}, bf16[1024,128]{1,0:T(8,128)(2,1)S(1)}, u32[]{:S(2)}, u32[]{:S(2)}) collective-permute-start(bf16[1024,128]{1,0:T(8,128)(2,1)S(1)} %get-tuple-element.91), channel_id=1, source_target_pairs={{0,14},{1,15},{2,0},{3,1},{4,2},{5,3},{6,4},{7,5},{8,6},{9,7},{10,... | collective-permute-start | bytes 786440 | tf_op jit(solution)/shard_map/ppermute | solution.py:281
  156.7 16.0 %collective-permute-start.6 = (bf16[512,128]{1,0:T(8,128)(2,1)S(1)}, bf16[512,128]{1,0:T(8,128)(2,1)S(1)}, u32[]{:S(2)}, u32[]{:S(2)}) collective-permute-start(bf16[512,128]{1,0:T(8,128)(2,1)S(1)} %get-tuple-element.67), channel_id=1, source_target_pairs={{0,4},{1,5},{2,6},{3,7},{4,8},{5,9},{6,10},{7,11},{8,12},{9,13},{1... | collective-permute-start | bytes 393224 | tf_op jit(solution)/shard_map/ppermute | solution.py:281
  160.9 50.8 %collective-permute-start.37 = (bf16[1024,128]{1,0:T(8,128)(2,1)S(1)}, bf16[1024,128]{1,0:T(8,128)(2,1)S(1)}, u32[]{:S(2)}, u32[]{:S(2)}) collective-permute-start(bf16[1024,128]{1,0:T(8,128)(2,1)S(1)} %get-tuple-element.103), channel_id=1, source_target_pairs={{0,2},{1,3},{2,4},{3,5},{4,6},{5,7},{6,8},{7,9},{8,10},{9,11},{10,... | collective-permute-start | bytes 786440 | tf_op jit(solution)/shard_map/ppermute | solution.py:281
  164.5 51.6 %collective-permute-start.38 = (bf16[1024,128]{1,0:T(8,128)(2,1)S(1)}, bf16[1024,128]{1,0:T(8,128)(2,1)S(1)}, u32[]{:S(2)}, u32[]{:S(2)}) collective-permute-start(bf16[1024,128]{1,0:T(8,128)(2,1)S(1)} %get-tuple-element.104), channel_id=1, source_target_pairs={{0,14},{1,15},{2,0},{3,1},{4,2},{5,3},{6,4},{7,5},{8,6},{9,7},{10,... | collective-permute-start | bytes 786440 | tf_op jit(solution)/shard_map/ppermute | solution.py:281
  164.5 60.9 %copy-start.1 = (f32[4,128,512]{2,1,0:T(8,128)S(1)}, f32[4,128,512]{2,1,0:T(8,128)}, u32[]{:S(2)}) copy-start(f32[4,128,512]{2,1,0:T(8,128)} %parent.1) | copy-start | bytes 3145732
  172.7 12.6 %collective-permute-start.7 = (bf16[512,128]{1,0:T(8,128)(2,1)S(1)}, bf16[512,128]{1,0:T(8,128)(2,1)S(1)}, u32[]{:S(2)}, u32[]{:S(2)}) collective-permute-start(bf16[512,128]{1,0:T(8,128)(2,1)S(1)} %get-tuple-element.68), channel_id=1, source_target_pairs={{0,8},{1,9},{2,10},{3,11},{4,12},{5,13},{6,14},{7,15},{8,0},{9,1},... | collective-permute-start | bytes 393224 | tf_op jit(solution)/shard_map/ppermute | solution.py:281
  177.3 13.1 %collective-permute-start.8 = (bf16[512,128]{1,0:T(8,128)(2,1)S(1)}, bf16[512,128]{1,0:T(8,128)(2,1)S(1)}, u32[]{:S(2)}, u32[]{:S(2)}) collective-permute-start(bf16[512,128]{1,0:T(8,128)(2,1)S(1)} %get-tuple-element.69), channel_id=1, source_target_pairs={{0,12},{1,13},{2,14},{3,15},{4,0},{5,1},{6,2},{7,3},{8,4},{9,5},{1... | collective-permute-start | bytes 393224 | tf_op jit(solution)/shard_map/ppermute | solution.py:281
  177.3 14.7 %collective-permute-start.17 = (bf16[512,128]{1,0:T(8,128)(2,1)S(1)}, bf16[512,128]{1,0:T(8,128)(2,1)S(1)}, u32[]{:S(2)}, u32[]{:S(2)}) collective-permute-start(bf16[512,128]{1,0:T(8,128)(2,1)S(1)} %get-tuple-element.80), channel_id=1, source_target_pairs={{0,4},{1,5},{2,6},{3,7},{4,8},{5,9},{6,10},{7,11},{8,12},{9,13},{1... | collective-permute-start | bytes 393224 | tf_op jit(solution)/shard_map/ppermute | solution.py:281
  185.3 35.9 %collective-permute-start.18 = (bf16[512,128]{1,0:T(8,128)(2,1)S(1)}, bf16[512,128]{1,0:T(8,128)(2,1)S(1)}, u32[]{:S(2)}, u32[]{:S(2)}) collective-permute-start(bf16[512,128]{1,0:T(8,128)(2,1)S(1)} %get-tuple-element.81), channel_id=1, source_target_pairs={{0,8},{1,9},{2,10},{3,11},{4,12},{5,13},{6,14},{7,15},{8,0},{9,1},... | collective-permute-start | bytes 393224 | tf_op jit(solution)/shard_map/ppermute | solution.py:281
  190.3 30.9 %collective-permute-start.19 = (bf16[512,128]{1,0:T(8,128)(2,1)S(1)}, bf16[512,128]{1,0:T(8,128)(2,1)S(1)}, u32[]{:S(2)}, u32[]{:S(2)}) collective-permute-start(bf16[512,128]{1,0:T(8,128)(2,1)S(1)} %get-tuple-element.82), channel_id=1, source_target_pairs={{0,12},{1,13},{2,14},{3,15},{4,0},{5,1},{6,2},{7,3},{8,4},{9,5},{1... | collective-permute-start | bytes 393224 | tf_op jit(solution)/shard_map/ppermute | solution.py:281
  192.0 31.5 %collective-permute-start.28 = (bf16[512,128]{1,0:T(8,128)(2,1)S(1)}, bf16[512,128]{1,0:T(8,128)(2,1)S(1)}, u32[]{:S(2)}, u32[]{:S(2)}) collective-permute-start(bf16[512,128]{1,0:T(8,128)(2,1)S(1)} %get-tuple-element.93), channel_id=1, source_target_pairs={{0,4},{1,5},{2,6},{3,7},{4,8},{5,9},{6,10},{7,11},{8,12},{9,13},{1... | collective-permute-start | bytes 393224 | tf_op jit(solution)/shard_map/ppermute | solution.py:281
  211.7 13.7 %collective-permute-start.29 = (bf16[512,128]{1,0:T(8,128)(2,1)}, bf16[512,128]{1,0:T(8,128)(2,1)S(1)}, u32[]{:S(2)}, u32[]{:S(2)}) collective-permute-start(bf16[512,128]{1,0:T(8,128)(2,1)} %get-tuple-element.94), channel_id=1, source_target_pairs={{0,8},{1,9},{2,10},{3,11},{4,12},{5,13},{6,14},{7,15},{8,0},{9,1},... | collective-permute-start | bytes 393224 | tf_op jit(solution)/shard_map/ppermute | solution.py:281
  216.0 9.4 %collective-permute-start.30 = (bf16[512,128]{1,0:T(8,128)(2,1)}, bf16[512,128]{1,0:T(8,128)(2,1)S(1)}, u32[]{:S(2)}, u32[]{:S(2)}) collective-permute-start(bf16[512,128]{1,0:T(8,128)(2,1)} %get-tuple-element.95), channel_id=1, source_target_pairs={{0,12},{1,13},{2,14},{3,15},{4,0},{5,1},{6,2},{7,3},{8,4},{9,5},{1... | collective-permute-start | bytes 393224 | tf_op jit(solution)/shard_map/ppermute | solution.py:281
  221.2 7.3 %collective-permute-start.39 = (bf16[512,128]{1,0:T(8,128)(2,1)}, bf16[512,128]{1,0:T(8,128)(2,1)S(1)}, u32[]{:S(2)}, u32[]{:S(2)}) collective-permute-start(bf16[512,128]{1,0:T(8,128)(2,1)} %get-tuple-element.106), channel_id=1, source_target_pairs={{0,4},{1,5},{2,6},{3,7},{4,8},{5,9},{6,10},{7,11},{8,12},{9,13},{1... | collective-permute-start | bytes 393224 | tf_op jit(solution)/shard_map/ppermute | solution.py:281
  221.2 10.7 %collective-permute-start.40 = (bf16[512,128]{1,0:T(8,128)(2,1)}, bf16[512,128]{1,0:T(8,128)(2,1)S(1)}, u32[]{:S(2)}, u32[]{:S(2)}) collective-permute-start(bf16[512,128]{1,0:T(8,128)(2,1)} %get-tuple-element.107), channel_id=1, source_target_pairs={{0,8},{1,9},{2,10},{3,11},{4,12},{5,13},{6,14},{7,15},{8,0},{9,1},... | collective-permute-start | bytes 393224 | tf_op jit(solution)/shard_map/ppermute | solution.py:281
  223.6 10.1 %collective-permute-start.41 = (bf16[512,128]{1,0:T(8,128)(2,1)}, bf16[512,128]{1,0:T(8,128)(2,1)}, u32[]{:S(2)}, u32[]{:S(2)}) collective-permute-start(bf16[512,128]{1,0:T(8,128)(2,1)} %get-tuple-element.108), channel_id=1, source_target_pairs={{0,12},{1,13},{2,14},{3,15},{4,0},{5,1},{6,2},{7,3},{8,4},{9,5},{1... | collective-permute-start | bytes 393224 | tf_op jit(solution)/shard_map/ppermute | solution.py:281
